TPU v7x, 8 devices: a whole 2x2x1 slice. The times are simulated.
8 devices in a mesh: dp: 1 (over z), tp: 2 (over y), sp: 4 (over x, core).
Axes of the slice: x: 2, y: 2, z: 1, core: 2. Of those that a mesh axis runs over, the one named last changes fastest.
Arguments:
- hidden: bfloat16 [256, 6144], P('dp')
- lat_cache: bfloat16 [256, 2048, 512], P('dp', 'sp')
- rope_cache: bfloat16 [256, 2048, 64], P('dp', 'sp')
- positions: int32 [256], P('dp')
- w_dq: bfloat16 [6144, 1536], replicated
- gain_q: bfloat16 [1536], replicated
- w_dkv: bfloat16 [6144, 576], replicated
- gain_kv: bfloat16 [512], replicated
- w_uq: bfloat16 [1536, 64, 192], P(None, 'tp')
- w_uk: bfloat16 [512, 64, 128], P(None, 'tp')
- w_uv: bfloat16 [512, 64, 128], P(None, 'tp')
- w_out: bfloat16 [8192, 6144], P('tp')
Outputs:
- output 1: bfloat16 [256, 6144], P('dp')
- output 2: bfloat16 [256, 2048, 512], P('dp', 'sp')
- output 3: bfloat16 [256, 2048, 64], P('dp', 'sp')
All inputs are finite; a program needn't handle non-finite values.
Results may differ from a plain program's by a relative error of at most 0.0116176.
Values sent between devices are 32-bit elements.
A program may use at most 1.75 GiB of HBM per device.

v0:
```python
import math
import jax
import jax.numpy as jnp
from jax import lax
from jax.sharding import PartitionSpec as P

EPSILON = 1e-6
ROPE_BASE = 50000.0
YARN_MSCALE = 1.0 + 0.1 * math.log(32.0)
MASK_VALUE = -1e30


def rms_norm(values, gain):
    vals32 = values.astype(jnp.float32)
    inv_rms = lax.rsqrt(jnp.mean(vals32 * vals32, axis=-1, keepdims=True) + EPSILON)
    return vals32 * inv_rms * gain.astype(jnp.float32)


def rope_tables(positions, rope_dim):
    half_dim = rope_dim // 2
    inv_freq = ROPE_BASE ** (-jnp.arange(half_dim).astype(jnp.float32) / half_dim)
    angles = positions.astype(jnp.float32)[:, None] * inv_freq[None, :]
    return jnp.cos(angles), jnp.sin(angles)


def rotate_pairs(values, cos_t, sin_t):
    half_dim = values.shape[-1] // 2
    first_half = values[..., :half_dim]
    second_half = values[..., half_dim:]
    return jnp.concatenate([first_half * cos_t - second_half * sin_t, second_half * cos_t + first_half * sin_t], axis=-1)


def project_inputs(hidden, positions, w_dq, gain_q, w_dkv, gain_kv, w_uq, w_uk):
    kv_rank = w_uk.shape[0]
    nope_dim = w_uk.shape[2]
    cos_t, sin_t = rope_tables(positions, w_uq.shape[2] - nope_dim)
    h_q = jnp.dot(hidden, w_dq, preferred_element_type=jnp.float32).astype(jnp.bfloat16)
    c_q = rms_norm(h_q, gain_q).astype(jnp.bfloat16)
    q_full = jnp.einsum('br,rhd->bhd', c_q, w_uq, preferred_element_type=jnp.float32).astype(jnp.bfloat16)
    q_rope = rotate_pairs(q_full[:, :, nope_dim:].astype(jnp.float32), cos_t[:, None, :], sin_t[:, None, :]).astype(jnp.bfloat16)
    q_abs = jnp.einsum('bhn,khn->bhk', q_full[:, :, :nope_dim], w_uk, preferred_element_type=jnp.float32).astype(jnp.bfloat16)
    kv_down = jnp.dot(hidden, w_dkv, preferred_element_type=jnp.float32).astype(jnp.bfloat16)
    lat_new = rms_norm(kv_down[:, :kv_rank], gain_kv).astype(jnp.bfloat16)
    rope_new = rotate_pairs(kv_down[:, kv_rank:].astype(jnp.float32), cos_t, sin_t).astype(jnp.bfloat16)
    return q_abs, q_rope, lat_new, rope_new


def solution(mesh):
    row_spec = P('dp', None)
    cache_spec = P('dp', 'sp', None)
    head_spec = P(None, 'tp', None)
    in_specs = (row_spec, cache_spec, cache_spec, P('dp'), P(), P(), P(), P(), head_spec, head_spec, head_spec, P('tp', None))
    out_specs = (row_spec, cache_spec, cache_spec)

    def local_step(hidden, lat_cache, rope_cache, positions, w_dq, gain_q, w_dkv, gain_kv, w_uq, w_uk, w_uv, w_out):
        rows_local = hidden.shape[0]
        seq_local = lat_cache.shape[1]
        score_scale = YARN_MSCALE ** 2 / math.sqrt(w_uq.shape[2])
        q_abs, q_rope, lat_new, rope_new = project_inputs(hidden, positions, w_dq, gain_q, w_dkv, gain_kv, w_uq, w_uk)
        slot_ids = lax.axis_index('sp') * seq_local + jnp.arange(seq_local)
        slot_hit = (slot_ids[None, :] == positions[:, None])[:, :, None]
        lat_all = jnp.where(slot_hit, lat_new[:, None, :], lat_cache)
        rope_all = jnp.where(slot_hit, rope_new[:, None, :], rope_cache)
        scores = (jnp.einsum('bhk,bsk->bhs', q_abs, lat_all, preferred_element_type=jnp.float32) + jnp.einsum('bhr,bsr->bhs', q_rope, rope_all, preferred_element_type=jnp.float32)) * score_scale
        key_valid = slot_ids[None, None, :] <= positions[:, None, None]
        scores = jnp.where(key_valid, scores, MASK_VALUE)
        max_global = lax.pmax(jnp.max(scores, axis=-1), 'sp')
        weights = jnp.exp(scores - max_global[:, :, None])
        lat_part = jnp.einsum('bhs,bsk->bhk', weights.astype(jnp.bfloat16), lat_all, preferred_element_type=jnp.float32)
        denominator, lat_sum = lax.psum((jnp.sum(weights, axis=-1), lat_part), 'sp')
        o_lat = (lat_sum / denominator[:, :, None]).astype(jnp.bfloat16)
        o_heads = jnp.einsum('bhk,khv->bhv', o_lat, w_uv, preferred_element_type=jnp.float32).astype(jnp.bfloat16)
        attn_part = jnp.dot(o_heads.reshape(rows_local, -1), w_out, preferred_element_type=jnp.float32)
        attn_out = lax.psum(attn_part, 'tp')
        return (hidden.astype(jnp.float32) + attn_out).astype(jnp.bfloat16), lat_all, rope_all

    return jax.shard_map(local_step, mesh=mesh, in_specs=in_specs, out_specs=out_specs, check_vma=False)
```

profile of v0, /device:TPU:0, one launch (start us, length us, event | category | flops | bytes accessed | tf_op | source)
XLA Modules:
  0.0 805.6 jit_solution(7750593443344497676)
XLA Ops:
  7.2 0.0 all-reduce.3.cloned.1.call-start
  7.2 0.0 copy-start.3
  7.2 0.0 copy-start.1
  7.3 6.1 convolution_convert_fusion.1
  13.4 0.1 fusion.19
  13.5 0.0 copy-done.3
  13.5 0.0 copy-done.1
  13.5 0.0 copy-start.4
  13.5 9.1 %multiply_reduce_fusion = (f32[256]{0:T(256)S(1)}, f32[256,1536]{1,0:T(8,128)S(1)}) fusion(bf16[256,6144]{1,0:T(8,128)(2,1)S(1)} %copy-done.1, bf16[6144,1536]{1,0:T(8,128)(2,1)} %param.16), kind=kOutput, calls=%fused_computation.21 | convolution fusion | flops 4833411072 | bytes 23593984 | tf_op jit(solution)/shard_map/dot_general | solution.py:37
  22.7 0.0 copy-done.4
  22.7 9.4 %fusion.16 = f32[256,6144]{0,1:S(1)} fusion(bf16[1536,6144]{0,1:T(8,128)(2,1)} %bitcast.24, f32[256,1536]{1,0:T(8,128)S(1)} %get-tuple-element.12, f32[1536]{0:T(1024)S(1)} %convert_element_type.76, f32[256]{0:T(256)S(1)} %add_rsqrt_fusion.1), kind=kOutput, calls=%fused_computation.27 | convolution fusion | flops 4833017856 | bytes 26745856
  32.1 0.4 convert_element_type.78
  32.5 0.0 copy-start
  32.5 0.0 copy-start.5
  32.6 0.2 slice_convert_fusion
  32.8 0.2 subtract_convert_fusion.1
  33.0 0.4 subtract_convert_fusion
  33.4 0.8 copy-done
  34.2 0.1 pad_maximum_fusion
  34.3 3.4 copy.21
  37.7 0.1 copy.20
  37.8 0.2 broadcast_compare_fusion.1
  38.0 0.0 copy-done.5
  38.1 0.1 fusion.21
  38.2 0.1 copy.19
  38.3 11.0 %fusion.8 = bf16[32,256,512]{2,1,0:T(8,128)(2,1)} fusion(bf16[512,32,128]{2,1,0:T(8,128)(2,1)} %param.21, bf16[256,32,192]{0,2,1:T(8,128)(2,1)} %copy-done), kind=kOutput, calls=%fused_computation.13 | convolution fusion | flops 1073741824 | bytes 14680064 | tf_op jit(solution)/shard_map/bhn,khn->bhk/dot_general | solution.py:41
  49.3 14.5 %broadcast_select_fusion.1 = bf16[256,512,64]{1,2,0:T(8,128)(2,1)} fusion(bf16[256,512,64]{1,2,0:T(8,128)(2,1)} %param.14, pred[256,512]{1,0:T(8,128)(4,1)S(1)} %get-tuple-element.8, bf16[256,64]{1,0:T(8,128)(2,1)S(1)} %copy.20), kind=kLoop, calls=%fused_computation.5 | loop fusion | flops 8388608 | bytes 33718272 | tf_op jit(solution)/shard_map/jit(_where)/select_n | solution.py:63
  63.8 13.9 %fusion.23 = f32[256,32,512]{2,1,0:T(8,128)} fusion(bf16[256,32,64]{2,1,0:T(8,128)(2,1)S(1)} %copy.21, bf16[256,512,64]{1,2,0:T(8,128)(2,1)} %broadcast_select_fusion.1), kind=kOutput, calls=%fused_computation.48 | convolution fusion | flops 536870912 | bytes 34603008 | tf_op jit(solution)/shard_map/bhr,bsr->bhs/dot_general | solution.py:64
  77.7 87.7 %broadcast_select_fusion = bf16[256,512,512]{2,1,0:T(8,128)(2,1)} fusion(bf16[256,512,512]{2,1,0:T(8,128)(2,1)} %param.13, pred[256,512]{1,0:T(8,128)(4,1)S(1)} %get-tuple-element.8, bf16[256,512]{1,0:T(8,128)(2,1)S(1)} %copy.19), kind=kLoop, calls=%fused_computation | loop fusion | flops 67108864 | bytes 268828672 | tf_op jit(solution)/shard_map/jit(_where)/select_n | solution.py:62
  165.4 73.0 %fusion.22 = (f32[256,32]{1,0:T(8,128)S(1)}, f32[256,32,512]{2,1,0:T(8,128)}) fusion(f32[256,32,512]{2,1,0:T(8,128)} %fusion.23, bf16[256,512,512]{2,1,0:T(8,128)(2,1)} %broadcast_select_fusion, bf16[32,256,512]{2,1,0:T(8,128)(2,1)} %fusion.8, pred[256,512]{1,0:T(8,128)(4,1)S(1)} %get-tuple-element.7), kind=kOutput, calls=%fused_computation.47 | convolution fusion | flops 4311736320 | bytes 176324608 | tf_op jit(solution)/shard_map/bhk,bsk->bhs/dot_general | solution.py:64
  238.5 15.0 %pmax.7 = f32[256,32]{1,0:T(8,128)S(1)} all-reduce(f32[256,32]{1,0:T(8,128)S(1)} %get-tuple-element.13), channel_id=1, replica_groups=mesh['dp'=1,'tp'=2,'sp'=4] {'sp'}, use_global_device_ids=true, to_apply=%region_3.4 | all-reduce | flops 8192 | bytes 65536 | tf_op jit(solution)/shard_map/pmax | solution.py:67
  253.5 53.9 %fusion.2 = f32[256,32,512]{2,1,0:T(8,128)} fusion(bf16[256,512,512]{2,1,0:T(8,128)(2,1)} %broadcast_select_fusion, f32[256,32,512]{2,1,0:T(8,128)} %get-tuple-element.14, f32[256,32]{1,0:T(8,128)S(1)} %pmax.7), kind=kOutput, calls=%fused_computation.8 | convolution fusion | flops 4303355904 | bytes 167804928 | tf_op jit(solution)/shard_map/bhs,bsk->bhk/dot_general | solution.py:69
  307.4 17.7 %copy.26 = f32[256,32,512]{2,0,1:T(8,128)} copy(f32[256,32,512]{2,1,0:T(8,128)} %fusion.2) | data formatting | bytes 33554432 | tf_op jit(solution)/shard_map/bhs,bsk->bhk/dot_general | solution.py:69
  325.1 0.0 all-reduce.3.cloned.1.call-update
  325.1 0.0 all-reduce.5.cloned.1.call-start
  325.1 7.6 fusion
  332.8 15.2 %psum.22 = f32[256,32]{1,0:T(8,128)S(1)} all-reduce(f32[256,32]{1,0:T(8,128)S(1)} %fusion), channel_id=1, replica_groups=mesh['dp'=1,'tp'=2,'sp'=4] {'sp'}, use_global_device_ids=true, to_apply=%region_6.7 | all-reduce | flops 8192 | bytes 65536 | tf_op jit(solution)/shard_map/psum | solution.py:70
  348.0 0.1 copy.22
  348.0 261.9 %all-reduce.3.cloned.1.call-done = f32[256,32,512]{2,0,1:T(8,128)} async-done(((f32[256,32,512]{2,0,1:T(8,128)}), f32[256,32,512]{2,0,1:T(8,128)}) %all-reduce.3.cloned.1.call-update) | async-done | bytes 16777232 | tf_op jit(solution)/shard_map/psum | solution.py:70
  609.9 13.0 %fusion.13 = bf16[32,256,128]{1,2,0:T(8,128)(2,1)S(1)} fusion(bf16[512,32,128]{2,1,0:T(8,128)(2,1)} %param.22, f32[256,32,512]{2,0,1:T(8,128)} %all-reduce.3.cloned.1.call-done, f32[256,32]{0,1:T(8,128)S(1)} %copy.22), kind=kOutput, calls=%fused_computation.19 | convolution fusion | flops 1083179008 | bytes 23101440 | tf_op jit(solution)/shard_map/bhk,khv->bhv/dot_general | solution.py:72
  622.9 22.7 %fusion.24 = f32[256,6144]{1,0:T(8,128)} fusion(bf16[256,4096]{0,1:T(8,128)(2,1)S(1)} %bitcast.23, bf16[4096,6144]{1,0:T(8,128)(2,1)} %param.23), kind=kOutput, calls=%fused_computation.49 | convolution fusion | flops 12884901888 | bytes 58720256 | tf_op jit(solution)/shard_map/dot_general | solution.py:73
  645.6 0.0 copy-start.2
  645.6 0.0 all-reduce.5.cloned.1.call-update
  645.7 147.6 %all-reduce.5.cloned.1.call-done = f32[256,6144]{1,0:T(8,128)} async-done(((f32[256,6144]{1,0:T(8,128)}), f32[256,6144]{1,0:T(8,128)}) %all-reduce.5.cloned.1.call-update) | async-done | bytes 6291472 | tf_op jit(solution)/shard_map/psum | solution.py:74
  793.2 0.0 copy-done.2
  793.2 5.3 add_convert_fusion
  (9 shorter events, 0.0 us)
Async XLA Ops:
  7.2 602.8 %all-reduce.3.cloned.1.call-start = ((), (), s32[]{:S(2)}) async-start(), calls=%async_computation | async-start | bytes 33554432 | tf_op jit(solution)/shard_map/psum | solution.py:70
  7.2 6.3 copy-start.3
  7.2 6.3 copy-start.1
  13.5 9.2 %copy-start.4 = (bf16[1536]{0:T(1024)(128)(2,1)S(1)}, bf16[1536]{0:T(1024)(128)(2,1)}, u32[]{:S(2)}) copy-start(bf16[1536]{0:T(1024)(128)(2,1)} %param.17) | copy-start | bytes 9220
  32.5 1.7 copy-start
  32.5 5.5 copy-start.5
  325.1 468.1 %all-reduce.5.cloned.1.call-start = ((), (), s32[]{:S(2)}) async-start(), calls=%async_computation.1 | async-start | bytes 12582912 | tf_op jit(solution)/shard_map/psum | solution.py:74
  645.6 147.6 %copy-start.2 = (bf16[256,6144]{1,0:T(8,128)(2,1)S(1)}, bf16[256,6144]{1,0:T(8,128)(2,1)}, u32[]{:S(2)}) copy-start(bf16[256,6144]{1,0:T(8,128)(2,1)} %param.12) | copy-start | bytes 9437188
Sparse Core Ops, SparseCore 0:
  325.2 284.6 all-reduce.2
  645.8 147.4 all-reduce.4
where the time goes:
time: 813 us; the launch traced here: 806 us
  waiting for transfers between devices  409 us (50%)
  matrix products  212 us (26%)
  other arithmetic  117 us (14%)
  blocking collectives  30.2 us (4%)
  local copies, waits for them, and re-layouts  22.2 us (3%)
  between operations  14.5 us (2%)
    psum x1, waiting for transfers between devices, local_step(): denominator, lat_sum = lax.psum((jnp.sum(weights, axis=-1), lat_part), 'sp')  262 us
    psum x1, waiting for transfers between devices, local_step(): attn_out = lax.psum(attn_part, 'tp')  148 us
    select_n x1, other arithmetic, local_step(): lat_all = jnp.where(slot_hit, lat_new[:, None, :], lat_cache)  87.7 us
    dot_general x1, matrix products, local_step(): jnp.einsum('bhk,bsk->bhs', q_abs, lat_all, preferred_element_type=jnp.flo...  73 us
    dot_general x1, matrix products, local_step(): jnp.einsum('bhs,bsk->bhk', weights.astype(jnp.bfloat16), lat_all, preferr...  53.9 us
    dot_general x1, matrix products, local_step(): jnp.dot(o_heads.reshape(rows_local, -1), w_out, preferred_element_type=jn...  22.7 us
    dot_general x1, local copies, waits for them, and re-layouts, local_step(): jnp.einsum('bhs,bsk->bhk', weights.astype(jnp.bfloat16), lat_all, preferr...  17.7 us
  transfers between devices with their start and end apart: 2, of which 2 were waited for; matrix products, arithmetic and copies ran while one was open for 1% of the time, Pallas kernels for 0%

commit v1 on v0

v1 whole, which is shorter than its diff:
```python
import functools
import math
import jax
import jax.numpy as jnp
from jax import lax
from jax.experimental import pallas as pl
from jax.experimental.pallas import tpu as pltpu
from jax.sharding import PartitionSpec as P

EPSILON = 1e-6
ROPE_BASE = 50000.0
YARN_MSCALE = 1.0 + 0.1 * math.log(32.0)
MASK_VALUE = -1e30
GROUP = 4
RING = 8
AHEAD = 4


def rms_norm(values, gain):
    vals32 = values.astype(jnp.float32)
    inv_rms = lax.rsqrt(jnp.mean(vals32 * vals32, axis=-1, keepdims=True) + EPSILON)
    return vals32 * inv_rms * gain.astype(jnp.float32)


def rope_tables(positions, rope_dim):
    half_dim = rope_dim // 2
    inv_freq = ROPE_BASE ** (-jnp.arange(half_dim).astype(jnp.float32) / half_dim)
    angles = positions.astype(jnp.float32)[:, None] * inv_freq[None, :]
    return jnp.cos(angles), jnp.sin(angles)


def rotate_pairs(values, cos_t, sin_t):
    half_dim = values.shape[-1] // 2
    first_half = values[..., :half_dim]
    second_half = values[..., half_dim:]
    return jnp.concatenate([first_half * cos_t - second_half * sin_t, second_half * cos_t + first_half * sin_t], axis=-1)


def heads_kernel(cq_ref, cos_ref, sin_ref, wuq_ref, wuk_ref, qa_ref, qr_ref, wide, lines, rlines):
    block = wuq_ref.shape[0]
    nope = wuk_ref.shape[2]
    rank = wuk_ref.shape[0]
    rdim = wuq_ref.shape[1] - nope
    hdim = rdim // 2
    wide[...] = wuk_ref[...].astype(jnp.float32)
    cq = cq_ref[...]
    cos = cos_ref[...]
    sin = sin_ref[...]
    for h in range(block):
        q = lax.dot_general(cq, wuq_ref[h], (((1,), (1,)), ((), ())), preferred_element_type=jnp.float32).astype(jnp.bfloat16)
        r = q[:, nope:].astype(jnp.float32)
        turned = jnp.concatenate([-r[:, hdim:], r[:, :hdim]], axis=1)
        rlines[:, h, :rdim] = r * cos + turned * sin
        wk = wide[:, h, :].astype(jnp.bfloat16)
        lines[:, h, :rank] = lax.dot_general(q[:, :nope], wk, (((1,), (1,)), ((), ())), preferred_element_type=jnp.float32)
    qa_ref[...] = lines[:, :, :rank].astype(jnp.bfloat16)
    qr_ref[...] = rlines[:, :, :rdim].astype(jnp.bfloat16)


def head_queries(cq, cos2, sin2, w_uq_t, w_uk):
    rows, qrank = cq.shape
    heads, qdim, _ = w_uq_t.shape
    rank, _, nope = w_uk.shape
    rdim = qdim - nope
    block = 8
    return pl.pallas_call(
        heads_kernel,
        grid=(heads // block,),
        in_specs=[
            pl.BlockSpec((rows, qrank), lambda i: (0, 0)),
            pl.BlockSpec((rows, rdim), lambda i: (0, 0)),
            pl.BlockSpec((rows, rdim), lambda i: (0, 0)),
            pl.BlockSpec((block, qdim, qrank), lambda i: (i, 0, 0)),
            pl.BlockSpec((rank, block, nope), lambda i: (0, i, 0)),
        ],
        out_specs=[
            pl.BlockSpec((rows, block, rank), lambda i: (0, i, 0)),
            pl.BlockSpec((rows, block, rdim), lambda i: (0, i, 0)),
        ],
        out_shape=[
            jax.ShapeDtypeStruct((rows, heads, rank), jnp.bfloat16),
            jax.ShapeDtypeStruct((rows, heads, rdim), jnp.bfloat16),
        ],
        scratch_shapes=[
            pltpu.VMEM((rank, block, nope), jnp.float32),
            pltpu.VMEM((rows, block, rank + 128), jnp.float32),
            pltpu.VMEM((rows, block, 128), jnp.float32),
        ],
        compiler_params=pltpu.CompilerParams(dimension_semantics=('arbitrary',), vmem_limit_bytes=48 * 2 ** 20),
        cost_estimate=pl.CostEstimate(flops=2 * rows * heads * (qdim * qrank + nope * rank), bytes_accessed=2 * heads * (qdim * qrank + nope * rank), transcendentals=0),
        name='head_queries',
    )(cq, cos2, sin2, w_uq_t, w_uk)


def project_inputs(hidden, positions, w_dq, gain_q, w_dkv, gain_kv, w_uq, w_uk):
    kv_rank = w_uk.shape[0]
    nope_dim = w_uk.shape[2]
    cos_t, sin_t = rope_tables(positions, w_uq.shape[2] - nope_dim)
    h_q = jnp.dot(hidden, w_dq, preferred_element_type=jnp.float32).astype(jnp.bfloat16)
    c_q = rms_norm(h_q, gain_q).astype(jnp.bfloat16)
    cos2 = jnp.concatenate([cos_t, cos_t], axis=1)
    sin2 = jnp.concatenate([sin_t, sin_t], axis=1)
    q_abs, q_rope = head_queries(c_q, cos2, sin2, jnp.transpose(w_uq, (1, 2, 0)), w_uk)
    kv_down = jnp.dot(hidden, w_dkv, preferred_element_type=jnp.float32).astype(jnp.bfloat16)
    lat_new = rms_norm(kv_down[:, :kv_rank], gain_kv).astype(jnp.bfloat16)
    rope_new = rotate_pairs(kv_down[:, kv_rank:].astype(jnp.float32), cos_t, sin_t).astype(jnp.bfloat16)
    return q_abs, q_rope, lat_new, rope_new


def attend_kernel(first, steps, scale, order_ref, pos_ref, where_ref, qa_ref, qr_ref, latn_ref, ropen_ref, lat_hbm, rope_hbm, *rest):
    uo_ref, us_ref, m_ref, l_ref, lat_out, rope_out, lat_buf, rope_buf, in_sem, out_sem = rest[-10:]
    t = pl.program_id(0)
    slots = lat_buf.shape[2]
    heads = qa_ref.shape[1]
    half = heads // 2
    start = where_ref[0]
    own = where_ref[1]

    def reads(step):
        ring = lax.rem(step, RING)
        out = []
        for g in range(GROUP):
            b = order_ref[first + step * GROUP + g]
            out.append(pltpu.make_async_copy(lat_hbm.at[b], lat_buf.at[ring, g], in_sem.at[ring, g, 0]))
            out.append(pltpu.make_async_copy(rope_hbm.at[b], rope_buf.at[ring, g], in_sem.at[ring, g, 1]))
        return out

    def writes(step):
        ring = lax.rem(step, RING)
        out = []
        for g in range(GROUP):
            b = order_ref[first + step * GROUP + g]
            out.append(pltpu.make_async_copy(lat_buf.at[ring, g], lat_out.at[b], out_sem.at[ring, g, 0]))
            out.append(pltpu.make_async_copy(rope_buf.at[ring, g], rope_out.at[b], out_sem.at[ring, g, 1]))
        return out

    @pl.when(t == 0)
    def _():
        for s in range(min(AHEAD, steps)):
            for c in reads(s):
                c.start()

    @pl.when(t >= RING - AHEAD)
    def _():
        for c in writes(t - (RING - AHEAD)):
            c.wait()

    @pl.when(t + AHEAD < steps)
    def _():
        for c in reads(t + AHEAD):
            c.start()

    for c in reads(t):
        c.wait()

    ring = lax.rem(t, RING)
    rows16 = lax.broadcasted_iota(jnp.int32, (16, 1), 0)
    lanes = lax.broadcasted_iota(jnp.int32, (1, 128), 1)
    rdim = ropen_ref.shape[1]
    eye = lax.broadcasted_iota(jnp.int32, (rdim, rdim), 0) == lax.broadcasted_iota(jnp.int32, (rdim, rdim), 1)
    for g in range(GROUP):
        i = first + t * GROUP + g
        s = pos_ref[i] - start
        inside = jnp.logical_and(s >= 0, s < slots)
        sc = jnp.where(inside, s, 0)
        r0 = pl.multiple_of((sc // 16) * 16, 16)
        hit = rows16 == jnp.where(inside, sc - r0, -1)
        blk = lat_buf[ring, g, pl.ds(r0, 16), :]
        new = latn_ref[pl.ds(i, 1), :]
        lat_buf[ring, g, pl.ds(r0, 16), :] = jnp.where(hit, new, blk.astype(jnp.float32)).astype(jnp.bfloat16)
        c0 = pl.multiple_of((sc // 128) * 128, 128)
        hitc = lanes == jnp.where(inside, sc - c0, -1)
        row = ropen_ref[pl.ds(i, 1), :]
        col = jnp.sum(jnp.where(eye, row, 0.0), axis=1, keepdims=True)
        rblk = rope_buf[ring, g, :, pl.ds(c0, 128)]
        rope_buf[ring, g, :, pl.ds(c0, 128)] = jnp.where(hitc, col, rblk.astype(jnp.float32)).astype(jnp.bfloat16)

    slot_ids = lax.broadcasted_iota(jnp.int32, (1, slots), 1) + start
    o0 = pl.multiple_of(own * half, half)
    o1 = pl.multiple_of((1 - own) * half, half)
    scores = []
    for g in range(GROUP):
        i = first + t * GROUP + g
        qa = jnp.concatenate([qa_ref[g, pl.ds(o0, half), :], qa_ref[g, pl.ds(o1, half), :]], axis=0)
        qr = jnp.concatenate([qr_ref[g, pl.ds(o0, half), :], qr_ref[g, pl.ds(o1, half), :]], axis=0)
        s = lax.dot_general(qa, lat_buf[ring, g], (((1,), (1,)), ((), ())), preferred_element_type=jnp.float32)
        s = (s + jnp.dot(qr, rope_buf[ring, g], preferred_element_type=jnp.float32)) * scale
        scores.append(jnp.where(slot_ids <= pos_ref[i], s, MASK_VALUE))
    ms = m_ref[...]
    ls = l_ref[...]
    for g in range(GROUP):
        i = first + t * GROUP + g
        m = jnp.max(scores[g], axis=1, keepdims=True)
        p = jnp.where(slot_ids <= pos_ref[i], jnp.exp(scores[g] - m), 0.0)
        l = jnp.sum(p, axis=1, keepdims=True)
        u = jnp.dot(p.astype(jnp.bfloat16), lat_buf[ring, g], preferred_element_type=jnp.float32)
        uo_ref[g] = u[:half]
        us_ref[g] = u[half:]
        j = t * GROUP + g
        ms = jnp.where(lanes == j, m, ms)
        ls = jnp.where(lanes == j, l, ls)
    m_ref[...] = ms
    l_ref[...] = ls

    for c in writes(t):
        c.start()

    @pl.when(t == steps - 1)
    def _():
        for s in range(max(0, steps - (RING - AHEAD)), steps):
            for c in writes(s):
                c.wait()


def attend_chunk(first, count, scale, order, pos, where, qa, qr, latn, ropen, lat, rope, prev):
    steps = count // GROUP
    heads, rank = qa.shape[1], qa.shape[2]
    rdim = qr.shape[2]
    slots = lat.shape[1]
    half = heads // 2
    base = first // GROUP
    any_spec = pl.BlockSpec(memory_space=pl.ANY)
    in_specs = [
        pl.BlockSpec((GROUP, heads, rank), lambda t, *_: (base + t, 0, 0)),
        pl.BlockSpec((GROUP, heads, rdim), lambda t, *_: (base + t, 0, 0)),
        pl.BlockSpec(latn.shape, lambda t, *_: (0, 0)),
        pl.BlockSpec(ropen.shape, lambda t, *_: (0, 0)),
        any_spec, any_spec,
    ]
    args = [order, pos, where, qa, qr, latn, ropen, lat, rope]
    aliases = {}
    if prev is not None:
        in_specs += [any_spec, any_spec]
        args += list(prev)
        aliases = {9: 4, 10: 5}
    return pl.pallas_call(
        functools.partial(attend_kernel, first, steps, scale),
        grid_spec=pltpu.PrefetchScalarGridSpec(
            num_scalar_prefetch=3,
            grid=(steps,),
            in_specs=in_specs,
            out_specs=[
                pl.BlockSpec((GROUP, half, rank), lambda t, *_: (t, 0, 0)),
                pl.BlockSpec((GROUP, half, rank), lambda t, *_: (t, 0, 0)),
                pl.BlockSpec((heads, 128), lambda t, *_: (0, 0)),
                pl.BlockSpec((heads, 128), lambda t, *_: (0, 0)),
                any_spec, any_spec,
            ],
            scratch_shapes=[
                pltpu.VMEM((RING, GROUP, slots, rank), jnp.bfloat16),
                pltpu.VMEM((RING, GROUP, rdim, slots), jnp.bfloat16),
                pltpu.SemaphoreType.DMA((RING, GROUP, 2)),
                pltpu.SemaphoreType.DMA((RING, GROUP, 2)),
            ],
        ),
        out_shape=[
            jax.ShapeDtypeStruct((count, half, rank), jnp.float32),
            jax.ShapeDtypeStruct((count, half, rank), jnp.float32),
            jax.ShapeDtypeStruct((heads, 128), jnp.float32),
            jax.ShapeDtypeStruct((heads, 128), jnp.float32),
            jax.ShapeDtypeStruct(lat.shape, jnp.bfloat16),
            jax.ShapeDtypeStruct(rope.shape, jnp.bfloat16),
        ],
        input_output_aliases=aliases,
        compiler_params=pltpu.CompilerParams(dimension_semantics=('arbitrary',), vmem_limit_bytes=56 * 2 ** 20),
        cost_estimate=pl.CostEstimate(
            flops=4 * count * heads * slots * rank * 16, bytes_accessed=count * slots * (rank + rdim) * 4, transcendentals=0),
        name='attend_chunk_%d' % first,
    )(*args)


def finish_kernel(place_ref, og_ref, o2_ref, hid_ref, w_hbm, out_ref, wbuf, part, got_c, sum_c, got_t, full, staged, o_got, w_sem, o_sem, c_sem, t_sem, ay_sem, ax_sem, af_sem, ac_sem):
    blocks, rows, width = part.shape
    half_blocks = blocks // 2
    r2, r4 = rows // 2, rows // 4
    depth = wbuf.shape[1]
    sp = lax.axis_index('sp')
    tp = lax.axis_index('tp')
    core = lax.rem(sp, 2)
    xpos = sp // 2
    sib = {'sp': sp + 1 - 2 * core}
    nbx = {'sp': lax.rem(sp + 2, 4)}
    nby = {'tp': 1 - tp}
    mesh_id = pl.DeviceIdType.MESH

    def remote(src, dst, sems, k, j, to):
        return pltpu.make_async_remote_copy(src_ref=src, dst_ref=dst, send_sem=sems.at[0, k, j], recv_sem=sems.at[1, k, j], device_id=to, device_id_type=mesh_id)

    def wcopy(j):
        col = lax.rem(j, half_blocks)
        return pltpu.make_async_copy(
            w_hbm.at[pl.ds(pl.multiple_of(core * depth, depth), depth), pl.ds(pl.multiple_of(col * width, width), width)],
            wbuf.at[lax.rem(j, wbuf.shape[0])], w_sem.at[lax.rem(j, wbuf.shape[0])])

    def spot(j, x, c, t):
        first = pl.multiple_of((j // half_blocks) * 4 * rows // 2 + ((x * 2 + c) * 2 + t) * r4, r4)
        return full.at[lax.rem(j, half_blocks), pl.ds(first, r4)]

    def send_o():
        return remote(o2_ref.at[pl.ds(rows, rows)], o_got, o_sem, 0, 0, nbx)

    def copy_c(j):
        return remote(part.at[j, pl.ds(pl.multiple_of((1 - core) * r2, r2), r2)], got_c.at[j], c_sem, 0, j, sib)

    def copy_t(j):
        return remote(sum_c.at[j, pl.ds(pl.multiple_of((1 - tp) * r4, r4), r4)], got_t.at[j], t_sem, 0, j, nby)

    def copy_ay(j):
        return remote(spot(j, xpos, core, tp), spot(j, xpos, core, tp), ay_sem, 0, j, nby)

    def copy_ax(j):
        return remote(spot(j, xpos, core, tp), spot(j, xpos, core, tp), ax_sem, 0, j, nbx)

    def copy_af(j):
        return remote(spot(j, xpos, core, 1 - tp), spot(j, xpos, core, 1 - tp), af_sem, 0, j, nbx)

    def copy_ac(j, k):
        x = xpos if k < 2 else 1 - xpos
        t = tp if k % 2 == 0 else 1 - tp
        return remote(spot(j, x, core, t), spot(j, x, core, t), ac_sem, k, j, sib)

    for j in range(wbuf.shape[0] - 1):
        wcopy(j).start()
    barrier = pltpu.get_barrier_semaphore()
    for to in (sib, nbx, nby):
        pl.semaphore_signal(barrier, inc=1, device_id=to, device_id_type=mesh_id)
    pl.semaphore_wait(barrier, 3)

    @pl.when(xpos == 0)
    def _():
        send_o().start()

    def body(i, carry):
        j = i

        @pl.when(j < blocks)
        def _():
            @pl.when(jnp.logical_and(j == half_blocks, xpos == 1))
            def _():
                send_o().wait_recv()

            wcopy(j).wait()
            w = wbuf.at[lax.rem(j, wbuf.shape[0])]

            @pl.when(j < half_blocks)
            def _():
                part[j] = jnp.dot(og_ref[...].astype(jnp.bfloat16), w[...], preferred_element_type=jnp.float32)

            @pl.when(j >= half_blocks)
            def _():
                o = jnp.where(xpos == 0, o2_ref[pl.ds(0, rows)], o_got[...])
                part[j] = jnp.dot(o.astype(jnp.bfloat16), w[...], preferred_element_type=jnp.float32)

            @pl.when(j + wbuf.shape[0] - 1 < blocks)
            def _():
                wcopy(j + wbuf.shape[0] - 1).start()

            copy_c(j).start()

        j1 = i - 1

        @pl.when(jnp.logical_and(j1 >= 0, j1 < blocks))
        def _():
            copy_c(j1).wait_recv()
            sum_c[j1] = part[j1, pl.ds(pl.multiple_of(core * r2, r2), r2)] + got_c[j1]
            copy_t(j1).start()

        j2 = i - 3

        @pl.when(jnp.logical_and(j2 >= 0, j2 < blocks))
        def _():
            copy_t(j2).wait_recv()
            first = pl.multiple_of((j2 // half_blocks) * 2 * rows + ((xpos * 2 + core) * 2 + tp) * r4, r4)
            full[lax.rem(j2, half_blocks), pl.ds(first, r4)] = sum_c[j2, pl.ds(pl.multiple_of(tp * r4, r4), r4)] + got_t[j2]
            copy_ay(j2).start()
            copy_ax(j2).start()
            copy_ac(j2, 0).start()

        j3 = i - 5

        @pl.when(jnp.logical_and(j3 >= 0, j3 < blocks))
        def _():
            copy_ay(j3).wait_recv()
            copy_af(j3).start()
            copy_ac(j3, 1).start()
            copy_ax(j3).wait_recv()
            copy_ac(j3, 2).start()

        j4 = i - 7

        @pl.when(jnp.logical_and(j4 >= 0, j4 < blocks))
        def _():
            copy_af(j4).wait_recv()
            copy_ac(j4, 3).start()

        j5 = i - 8

        @pl.when(jnp.logical_and(j5 >= 0, j5 < blocks))
        def _():
            for k in range(4):
                copy_ac(j5, k).wait_recv()

        @pl.when(jnp.logical_and(j5 >= half_blocks, j5 < blocks))
        def _():
            cb = j5 - half_blocks
            cols = pl.ds(pl.multiple_of(cb * width, width), width)
            staged[...] = full[cb]

            def emit(q, carry):
                b = pl.multiple_of(q * 16, 16)
                lines = [staged[pl.ds(place_ref[b + r], 1), :] for r in range(16)]
                y = jnp.concatenate(lines, axis=0)
                out_ref[pl.ds(b, 16), cols] = (hid_ref[pl.ds(b, 16), cols].astype(jnp.float32) + y).astype(jnp.bfloat16)
                return carry

            lax.fori_loop(0, out_ref.shape[0] // 16, emit, 0)

        return carry

    lax.fori_loop(0, blocks + 8, body, 0)

    def drain(j, carry):
        copy_c(j).wait_send()
        copy_t(j).wait_send()
        copy_ay(j).wait_send()
        copy_ax(j).wait_send()
        copy_af(j).wait_send()
        for k in range(4):
            copy_ac(j, k).wait_send()
        return carry

    lax.fori_loop(0, blocks, drain, 0)

    @pl.when(xpos == 0)
    def _():
        send_o().wait_send()


def finish(place, og, o2, hidden, w_out, blocks):
    rows, depth = og.shape
    batch, dmodel = hidden.shape
    width = dmodel // (blocks // 2)
    vmem = pl.BlockSpec(memory_space=pltpu.VMEM)
    ring = 4
    return pl.pallas_call(
        finish_kernel,
        in_specs=[pl.BlockSpec(memory_space=pltpu.SMEM), vmem, vmem, vmem, pl.BlockSpec(memory_space=pl.ANY)],
        out_specs=vmem,
        out_shape=jax.ShapeDtypeStruct((batch, dmodel), jnp.bfloat16),
        scratch_shapes=[
            pltpu.VMEM((ring, depth, width), jnp.bfloat16),
            pltpu.VMEM((blocks, rows, width), jnp.float32),
            pltpu.VMEM((blocks, rows // 2, width), jnp.float32),
            pltpu.VMEM((blocks, rows // 2, width), jnp.float32),
            pltpu.VMEM((blocks, rows // 4, width), jnp.float32),
            pltpu.VMEM((blocks // 2, batch, width), jnp.float32),
            pltpu.VMEM((batch, width), jnp.float32),
            pltpu.VMEM((rows, depth), jnp.float32),
            pltpu.SemaphoreType.DMA((ring,)),
            pltpu.SemaphoreType.DMA((2, 1, 1)),
            pltpu.SemaphoreType.DMA((2, 1, blocks)),
            pltpu.SemaphoreType.DMA((2, 1, blocks)),
            pltpu.SemaphoreType.DMA((2, 1, blocks)),
            pltpu.SemaphoreType.DMA((2, 1, blocks)),
            pltpu.SemaphoreType.DMA((2, 1, blocks)),
            pltpu.SemaphoreType.DMA((2, 4, blocks)),
        ],
        compiler_params=pltpu.CompilerParams(collective_id=1, has_side_effects=True, vmem_limit_bytes=60 * 2 ** 20),
        name='finish',
    )(place, og, o2, hidden, w_out)


def pair_kernel(m0_ref, l0_ref, m1_ref, l1_ref, uo_hbm, us_hbm, u_ref, m_ref, l_ref, got, own, mg, lg, ml_sem, d_sem, o_sem):
    blocks, rows = own.shape[0], own.shape[1]
    heads = own.shape[2]
    sp = lax.axis_index('sp')
    sib = {'sp': sp + 1 - 2 * lax.rem(sp, 2)}
    mesh_id = pl.DeviceIdType.MESH

    def remote(src, dst, sems, j):
        return pltpu.make_async_remote_copy(src_ref=src, dst_ref=dst, send_sem=sems.at[0, j], recv_sem=sems.at[1, j], device_id=sib, device_id_type=mesh_id)

    def mine(j):
        return pltpu.make_async_copy(uo_hbm.at[pl.ds(j * rows, rows)], own.at[j], o_sem.at[j])

    def theirs(j):
        return remote(us_hbm.at[pl.ds(j * rows, rows)], got.at[j], d_sem, j)

    barrier = pltpu.get_barrier_semaphore()
    pl.semaphore_signal(barrier, inc=1, device_id=sib, device_id_type=mesh_id)
    for j in range(blocks):
        mine(j).start()
    pl.semaphore_wait(barrier, 1)
    cm = remote(m1_ref, mg, ml_sem, 0)
    cl = remote(l1_ref, lg, ml_sem, 1)
    cm.start()
    cl.start()
    for j in range(blocks):
        theirs(j).start()
    cm.wait()
    cl.wait()
    m0, m1 = m0_ref[...], mg[...]
    m = jnp.maximum(m0, m1)
    a0 = jnp.exp(m0 - m)
    a1 = jnp.exp(m1 - m)
    m_ref[...] = m
    l_ref[...] = l0_ref[...] * a0 + lg[...] * a1
    lanes = lax.broadcasted_iota(jnp.int32, (1, 128), 1)

    def body(j, carry):
        mine(j).wait()
        theirs(j).wait_recv()
        for r in range(rows):
            hit = lanes == j * rows + r
            c0 = jnp.sum(jnp.where(hit, a0, 0.0), axis=1, keepdims=True)
            c1 = jnp.sum(jnp.where(hit, a1, 0.0), axis=1, keepdims=True)
            u_ref[j * rows + r] = own[j, r] * c0 + got[j, r] * c1
        return carry

    lax.fori_loop(0, blocks, body, 0)

    def drain(j, carry):
        theirs(j).wait_send()
        return carry

    lax.fori_loop(0, blocks, drain, 0)


def pair_merge(m, l, uo, us, tag):
    count, half, rank = uo.shape
    rows = 8
    blocks = count // rows
    vmem = pl.BlockSpec(memory_space=pltpu.VMEM)
    any_spec = pl.BlockSpec(memory_space=pl.ANY)
    return pl.pallas_call(
        pair_kernel,
        in_specs=[vmem, vmem, vmem, vmem, any_spec, any_spec],
        out_specs=[vmem, vmem, vmem],
        out_shape=[
            jax.ShapeDtypeStruct((count, half, rank), jnp.float32),
            jax.ShapeDtypeStruct((half, 128), jnp.float32),
            jax.ShapeDtypeStruct((half, 128), jnp.float32),
        ],
        scratch_shapes=[
            pltpu.VMEM((blocks, rows, half, rank), jnp.float32),
            pltpu.VMEM((blocks, rows, half, rank), jnp.float32),
            pltpu.VMEM((half, 128), jnp.float32),
            pltpu.VMEM((half, 128), jnp.float32),
            pltpu.SemaphoreType.DMA((2, 2)),
            pltpu.SemaphoreType.DMA((2, blocks)),
            pltpu.SemaphoreType.DMA((blocks,)),
        ],
        compiler_params=pltpu.CompilerParams(collective_id=tag, has_side_effects=True, vmem_limit_bytes=60 * 2 ** 20),
        name='pair_merge_%d' % tag,
    )(m[:half], l[:half], m[half:], l[half:], uo, us)


def merge(m0, l0, u0, m1, l1, u1):
    m = jnp.maximum(m0, m1)
    a0 = jnp.exp(m0 - m)
    a1 = jnp.exp(m1 - m)
    return m, l0 * a0 + l1 * a1, u0 * a0[:, :, None] + u1 * a1[:, :, None]


def solution(mesh):
    row_spec = P('dp', None)
    cache_spec = P('dp', 'sp', None)
    head_spec = P(None, 'tp', None)
    in_specs = (row_spec, cache_spec, cache_spec, P('dp'), P(), P(), P(), P(), head_spec, head_spec, head_spec, P('tp', None))
    out_specs = (row_spec, cache_spec, cache_spec)
    sibling = [(0, 1), (1, 0), (2, 3), (3, 2)]
    across = [(0, 2), (2, 0), (1, 3), (3, 1)]

    def local_step(hidden, lat_cache, rope_cache, positions, w_dq, gain_q, w_dkv, gain_kv, w_uq, w_uk, w_uv, w_out):
        rows = hidden.shape[0]
        slots = lat_cache.shape[1]
        heads = w_uq.shape[1]
        half = heads // 2
        scale = YARN_MSCALE ** 2 / math.sqrt(w_uq.shape[2])
        sp = lax.axis_index('sp')
        core = sp % 2
        xpos = sp // 2
        ids = jnp.arange(rows, dtype=jnp.int32)
        ahead = (positions[None, :] > positions[:, None]) | ((positions[None, :] == positions[:, None]) & (ids[None, :] < ids[:, None]))
        rank_of = jnp.sum(ahead.astype(jnp.int32), axis=1)
        pick = rank_of[None, :] == ids[:, None]
        order = jnp.sum(jnp.where(pick, ids[None, :], 0), axis=1)
        pos = jnp.sum(jnp.where(pick, positions[None, :], 0), axis=1)
        hid = jnp.dot((order[:, None] == ids[None, :]).astype(jnp.bfloat16), hidden, preferred_element_type=jnp.float32).astype(jnp.bfloat16)
        q_abs, q_rope, lat_new, rope_new = project_inputs(hid, pos, w_dq, gain_q, w_dkv, gain_kv, w_uq, w_uk)
        latn = lat_new.astype(jnp.float32)
        ropen = rope_new.astype(jnp.float32)
        rope_t = jnp.swapaxes(rope_cache, 1, 2)
        where = jnp.stack([sp * slots, core]).astype(jnp.int32)

        half_rows = rows // 2
        own_rows = rows // 4
        prev = None
        parts = []
        for g in range(2):
            if g == 1:
                tied = lax.optimization_barrier((where, keep, send))
                where, keep, send = tied
            uo, us, m, l, lo, ro = attend_chunk(g * half_rows, half_rows, scale, order, pos, where, q_abs, q_rope, latn, ropen, lat_cache, rope_t, prev)
            prev = (lo, ro)
            u, m, l = pair_merge(m, l, uo, us, 2 + g)
            m, l = m[:, :half_rows].T, l[:, :half_rows].T
            if g == 0:
                keep = [lax.dynamic_slice_in_dim(v, xpos * own_rows, own_rows, 0) for v in (m, l, u)]
                send = [lax.dynamic_slice_in_dim(v, (1 - xpos) * own_rows, own_rows, 0) for v in (m, l, u)]
        got = lax.ppermute(send, 'sp', across)
        _, l1, u1 = merge(*keep, *got)
        lat1 = (u1 / l1[:, :, None]).astype(jnp.bfloat16)
        lat_out, rope_out = prev[0], jnp.swapaxes(prev[1], 1, 2)

        def near(args):
            _, l, u = args
            return (u / jnp.where(l > 0, l, 1.0)[:, :, None]).astype(jnp.bfloat16)

        def far(args):
            got = lax.ppermute(list(args), 'sp', across)
            return near(merge(*args, *got))

        lat2 = lax.cond(pos[half_rows] >= 2 * slots, far, near, (m, l, u))
        w_uv_own = lax.dynamic_slice_in_dim(w_uv, core * half, half, 1)
        og = jnp.einsum('bhk,khv->bhv', lat1, w_uv_own, preferred_element_type=jnp.float32).reshape(own_rows, -1)
        o2 = jnp.einsum('bhk,khv->bhv', lat2, w_uv_own, preferred_element_type=jnp.float32).reshape(half_rows, -1)
        r = rank_of % half_rows
        x, k = r // own_rows, r % own_rows
        quarter = own_rows // 4
        c, t = k // (2 * quarter), (k // quarter) % 2
        place = (rank_of // half_rows) * half_rows + ((x * 2 + c) * 2 + t) * quarter + k % quarter
        out = finish(place.astype(jnp.int32), og, o2, hidden, w_out, 12)
        return out, lat_out, rope_out

    return jax.shard_map(local_step, mesh=mesh, in_specs=in_specs, out_specs=out_specs, check_vma=False)
```

time: 813 us -> 293 us (0.36)
  waiting for transfers between devices: 409 us -> 0.01 us
  Pallas kernels: 0 us -> 228 us
  matrix products: 212 us -> 24 us
  other arithmetic: 117 us -> 9.38 us
  blocking collectives: 30.2 us -> 0 us
  between operations: 14.5 us -> 1.65 us
    psum x2 -> x0, waiting for transfers between devices: 409 us -> none  [the longest x1 262 us: local_step(): denominator, lat_sum = lax.psum((jnp.sum(weights, axis=-1), lat_part), 'sp')]
    pallas_call x0 -> x6, Pallas kernels: none -> 228 us  [the longest x2 120 us: attend_chunk(): pl.pallas_call(functools.partial(attend_kernel, first, steps, scale), gri...]
    dot_general x6 -> x3, matrix products: 188 us -> 7.89 us  [the longest x1 3.06 us: local_step(): jnp.einsum('bhk,khv->bhv', lat2, w_uv_own, preferred_element_type=jnp.flo...]
    select_n x2 -> x1, other arithmetic: 102 us -> 0.01 us  [near(): return (u / jnp.where(l > 0, l, 1.0)[:, :, None]).astype(jnp.bfloat16)]
    dot_general x1 -> x0, local copies, waits for them, and re-layouts: 17.7 us -> none  [local_step(): jnp.einsum('bhs,bsk->bhk', weights.astype(jnp.bfloat16), lat_all, preferr...]
    psum x1 -> x0, blocking collectives: 15.2 us -> none  [local_step(): denominator, lat_sum = lax.psum((jnp.sum(weights, axis=-1), lat_part), 'sp')]
    pmax x1 -> x0, blocking collectives: 15 us -> none  [local_step(): max_global = lax.pmax(jnp.max(scores, axis=-1), 'sp')]
    unnamed x1 -> x0, matrix products: 9.38 us -> none
  transfers between devices with their start and end apart: 2 -> 3, of which waited for: 2 -> 0; matrix products, arithmetic and copies ran while one was open for 1% -> 4% of each run, Pallas kernels for 0% -> 24%
where the time goes in v1:
time: 293 us; the launch traced here: 292 us
  Pallas kernels  228 us (78%)
  matrix products  24 us (8%)
  local copies, waits for them, and re-layouts  23.3 us (8%)
  other arithmetic  9.38 us (3%)
  starting transfers between devices  5.04 us (2%)
    pallas_call x2, Pallas kernels, attend_chunk(): pl.pallas_call(functools.partial(attend_kernel, first, steps, scale), gri...  120 us
    pallas_call x1, Pallas kernels, finish(): pl.pallas_call(finish_kernel, in_specs=[pl.BlockSpec(memory_space=pltpu.S...  55.8 us
    pallas_call x1, Pallas kernels, head_queries(): pl.pallas_call(heads_kernel, grid=(heads // block,), in_specs=[pl.BlockSp...  30.3 us
    pallas_call x2, Pallas kernels, pair_merge(): pl.pallas_call(pair_kernel, in_specs=[vmem, vmem, vmem, vmem, any_spec, a...  21.6 us
    dot_general x1, matrix products, project_inputs(): jnp.dot(hidden, w_dq, preferred_element_type=jnp.float32)  10.5 us
    unnamed x27, local copies, waits for them, and re-layouts  6.89 us
    dynamic_slice x3, local copies, waits for them, and re-layouts, local_step(): lax.dynamic_slice_in_dim(v, (1 - xpos) * own_rows, own_rows, 0)  5.92 us
  transfers between devices with their start and end apart: 3, of which 0 were waited for; matrix products, arithmetic and copies ran while one was open for 4% of the time, Pallas kernels for 24%

profile of v1, /device:TPU:0, one launch (start us, length us, event | category | flops | bytes accessed | tf_op | source)
XLA Modules:
  0.0 291.8 jit_solution(6782321599455300702)
XLA Ops:
  0.7 0.9 convert_reduce_fusion
  1.6 0.0 copy-start.7
  1.6 0.8 select_reduce_fusion
  2.4 0.0 copy-done.7
  2.4 0.0 copy-start.6
  2.5 0.0 copy-start.9
  2.5 2.9 convolution_convert_fusion
  5.4 0.0 copy-done.6
  5.4 5.6 %convolution_convert_fusion.2 = bf16[256,576]{1,0:T(8,128)(2,1)S(1)} fusion(bf16[256,6144]{1,0:T(8,128)(2,1)S(1)} %convolution_convert_fusion, bf16[6144,576]{0,1:T(8,128)(2,1)} %param.20), kind=kOutput, calls=%fused_computation.19 | convolution fusion | flops 1812086784 | bytes 10518528 | tf_op jit(solution)/shard_map/dot_general | solution.py:104
  11.0 0.0 copy-start.5
  11.1 0.7 copy-done.5
  11.8 0.1 fusion.12
  11.9 0.0 copy-start.11
  11.9 0.0 copy-start.12
  12.0 10.5 %multiply_reduce_fusion = (f32[256]{0:T(256)S(1)}, f32[256,1536]{1,0:T(8,128)}) fusion(bf16[256,6144]{1,0:T(8,128)(2,1)S(1)} %convolution_convert_fusion, bf16[6144,1536]{1,0:T(8,128)(2,1)} %param.18), kind=kOutput, calls=%fused_computation.17 | convolution fusion | flops 4833411072 | bytes 23593984 | tf_op jit(solution)/shard_map/dot_general | solution.py:99
  22.4 0.0 copy-done.11
  22.5 0.0 copy-done.9
  22.5 0.0 copy-done.12
  22.5 0.7 pad_add_fusion.where_ref
  23.2 0.6 subtract_convert_fusion
  23.8 0.1 pad_maximum_fusion
  23.9 1.9 fusion.15.latn_ref
  25.8 0.7 maximum_convert_fusion.ropen_ref
  26.5 0.0 copy-done.4
  26.6 0.2 multiply_convert_fusion.cq_ref
  26.8 30.3 %head_queries.1 = (bf16[256,32,512]{2,1,0:T(8,128)(2,1)}, bf16[256,32,64]{2,1,0:T(8,128)(2,1)S(1)}) custom-call(bf16[256,1536]{1,0:T(8,128)(2,1)S(1)} %multiply_convert_fusion.cq_ref, f32[256,64]{1,0:T(8,128)S(1)} %get-tuple-element.107.cos_ref, f32[256,64]{1,0:T(8,128)S(1)} %get-tuple-element.108.sin_ref, bf16[32,192,1536]{2,1,0:T(8,128)(2,1)} %bitcast.30, ...), custom_call_target="tpu_custom_call" | custom-call | flops 5905580032 | bytes 23068672 | tf_op jit(solution)/shard_map/head_queries/pallas_call | solution.py:66
  57.1 1.3 copy-done
  58.4 60.0 %attend_chunk_0.1 = (f32[128,16,512]{2,1,0:T(8,128)}, f32[128,16,512]{2,1,0:T(8,128)}, f32[32,128]{1,0:T(8,128)}, f32[32,128]{1,0:T(8,128)}, bf16[256,512,512]{2...) custom-call(s32[256]{0:T(256)} %copy-done.6, s32[256]{0:T(256)} %copy-done.9, s32[2]{0:T(128)} %pad_add_fusion.where_ref, ...), custom_call_target="tpu_custom_call" | custom-call | flops 68719476736 | bytes 150994944 | tf_op jit(solution)/shard_map/attend_chunk_0/pallas_call | solution.py:236
  118.4 1.3 fusion.31
  119.8 1.3 fusion.30
  121.1 11.0 %pair_merge_2.1 = (f32[128,16,512]{2,1,0:T(8,128)}, f32[16,128]{1,0:T(8,128)}, f32[16,128]{1,0:T(8,128)}) custom-call(f32[16,128]{1,0:T(8,128)} %get-tuple-element.98.m0_ref, f32[16,128]{1,0:T(8,128)} %get-tuple-element.96.l0_ref, f32[16,128]{1,0:T(8,128)} %get-tuple-element.97.m1_ref, f32[16,128]{1,0:T(8,128)} %get-tuple-element.95.l1_ref, ...), custom_call_target="tpu_custom_call" | custom-call | tf_op jit(solution)/shard_map/pair_merge_2/pallas_call | solution.py:535
  132.1 0.9 dynamic-slice_bitcast_fusion.1
  132.9 0.8 dynamic-slice_bitcast_fusion
  133.8 4.2 %constant_dynamic-slice_fusion = (f32[64,16,512]{2,1,0:T(8,128)}, f32[64,16,512]{2,1,0:T(8,128)S(1)}) fusion(f32[128,16,512]{2,1,0:T(8,128)} %get-tuple-element.58, s32[]{:T(128)S(6)} %select_n.83, s32[]{:T(128)S(6)} %select_n.82), kind=kLoop, calls=%fused_computation.65 | loop fusion | bytes 8388616 | tf_op jit(solution)/shard_map/dynamic_slice | solution.py:610
  138.0 3.0 %collective-permute-start.4 = (f32[64,16,512]{2,1,0:T(8,128)}, f32[64,16,512]{2,1,0:T(8,128)}, u32[]{:S(2)}, u32[]{:S(2)}) collective-permute-start(f32[64,16,512]{2,1,0:T(8,128)} %get-tuple-element.62), channel_id=1, source_target_pairs={{0,2},{2,0},{1,3},{3,1},{4,6},{6,4},{5,7},{7,5}} | collective-permute-start | bytes 6291464 | tf_op jit(solution)/shard_map/ppermute | solution.py:611
  141.0 0.0 collective-permute-start.5
  141.0 60.3 %attend_chunk_128.1 = (f32[128,16,512]{2,1,0:T(8,128)}, f32[128,16,512]{2,1,0:T(8,128)}, f32[32,128]{1,0:T(8,128)}, f32[32,128]{1,0:T(8,128)}, bf16[256,512,512]...) custom-call(s32[256]{0:T(256)} %copy-done.6, s32[256]{0:T(256)} %copy-done.9, ...), custom_call_target="tpu_custom_call", output_to_operand_aliasing={{4}: (9, {}), {5}: (10, {})} | custom-call | flops 68719476736 | bytes 150994944 | tf_op jit(solution)/shard_map/attend_chunk_128/pallas_call | solution.py:236
  201.3 1.3 fusion.29
  202.7 0.0 copy-done.10
  202.7 0.6 slice.47
  203.9 1.3 fusion.28
  205.2 10.6 %pair_merge_3.1 = (f32[128,16,512]{2,1,0:T(8,128)}, f32[16,128]{1,0:T(8,128)S(1)}, f32[16,128]{1,0:T(8,128)S(1)}) custom-call(f32[16,128]{1,0:T(8,128)} %get-tuple-element.94.m0_ref, f32[16,128]{1,0:T(8,128)} %get-tuple-element.92.l0_ref, f32[16,128]{1,0:T(8,128)} %get-tuple-element.93.m1_ref, f32[16,128]{1,0:T(8,128)} %get-tuple-element.91.l1_ref, ...), custom_call_target="tpu_custom_call" | custom-call | tf_op jit(solution)/shard_map/pair_merge_3/pallas_call | solution.py:535
  215.9 0.2 conditional.2
  216.1 2.0 collective-permute-start.3
  218.2 0.1 copy.53
  218.3 2.1 constant_dynamic-slice_fusion.2
  220.4 0.0 copy-start.2
  220.4 0.7 copy-done.1
  221.1 0.4 divide_convert_fusion
  221.4 0.3 copy-done.2
  221.7 3.1 %fusion.3 = f32[16,128,128]{2,1,0:T(8,128)S(1)} fusion(bf16[128,16,512]{2,1,0:T(8,128)(2,1)S(1)} %divide_convert_fusion, bf16[512,16,128]{2,1,0:T(8,128)(2,1)S(1)} %constant_dynamic-slice_fusion.2), kind=kOutput, calls=%fused_computation.10 | convolution fusion | flops 268435456 | bytes 5242880 | tf_op jit(solution)/shard_map/bhk,khv->bhv/dot_general | solution.py:627
  224.8 0.6 fusion.22.place_ref
  225.4 1.4 copy.59.o2_ref
  226.8 0.0 collective-permute-done.5
  226.8 0.0 collective-permute-done.3
  226.8 0.1 copy.50
  226.9 0.1 copy.49
  227.0 0.1 copy.48
  227.0 0.0 collective-permute-done.4
  227.1 2.2 divide_convert_fusion.1
  229.3 1.9 fusion.8
  231.2 0.8 copy.73
  232.0 55.8 %finish.1 = bf16[256,6144]{1,0:T(8,128)(2,1)} custom-call(s32[256]{0:T(256)} %fusion.22.place_ref, f32[64,2048]{1,0:T(8,128)} %bitcast.34, f32[128,2048]{1,0:T(8,128)} %copy.59.o2_ref, bf16[256,6144]{1,0:T(8,128)(2,1)} %hid_ref.1, bf16[4096,6144]{1,0:T(8,128)(2,1)} %w_hbm.1), custom_call_target="tpu_custom_call" | custom-call | tf_op jit(solution)/shard_map/finish/pallas_call | solution.py:445
  287.9 3.9 %copy.81 = bf16[256,6144]{1,0:T(8,128)(2,1)} copy(bf16[256,6144]{1,0:T(8,128)(2,1)} %finish.1) | data formatting | bytes 6291456
  (17 shorter events, 0.1 us)
Async XLA Ops:
  1.6 0.8 copy-start.7
  2.4 2.9 %copy-start.6 = (s32[256]{0:T(256)}, s32[256]{0:T(256)S(1)}, u32[]{:S(2)}) copy-start(s32[256]{0:T(256)S(1)} %get-tuple-element.80.order_ref) | copy-start | bytes 3076
  2.5 20.0 %copy-start.9 = (s32[256]{0:T(256)}, s32[256]{0:T(256)S(1)}, u32[]{:S(2)}) copy-start(s32[256]{0:T(256)S(1)} %get-tuple-element.79.pos_ref) | copy-start | bytes 3076
  11.0 0.7 copy-start.5
  11.9 10.5 %copy-start.11 = (bf16[1536]{0:T(1024)(128)(2,1)S(1)}, bf16[1536]{0:T(1024)(128)(2,1)}, u32[]{:S(2)}) copy-start(bf16[1536]{0:T(1024)(128)(2,1)} %param.19) | copy-start | bytes 9220
  11.9 10.5 %copy-start.12 = (bf16[512]{0:T(512)(128)(2,1)S(1)}, bf16[512]{0:T(512)(128)(2,1)}, u32[]{:S(2)}) copy-start(bf16[512]{0:T(512)(128)(2,1)} %param.21) | copy-start | bytes 3076
  22.4 4.1 %copy-start.4 = (f32[256,1536]{1,0:T(8,128)S(1)}, f32[256,1536]{1,0:T(8,128)}, u32[]{:S(2)}) copy-start(f32[256,1536]{1,0:T(8,128)} %get-tuple-element.106) | copy-start | bytes 4718596
  57.1 1.3 copy-start
  138.0 89.1 %collective-permute-start.4 = (f32[64,16,512]{2,1,0:T(8,128)}, f32[64,16,512]{2,1,0:T(8,128)}, u32[]{:S(2)}, u32[]{:S(2)}) collective-permute-start(f32[64,16,512]{2,1,0:T(8,128)} %get-tuple-element.62), channel_id=1, source_target_pairs={{0,2},{2,0},{1,3},{3,1},{4,6},{6,4},{5,7},{7,5}} | collective-permute-start | bytes 6291464 | tf_op jit(solution)/shard_map/ppermute | solution.py:611
  141.0 85.8 %collective-permute-start.5 = (f32[64,16]{0,1:T(8,128)S(1)}, f32[64,16]{0,1:T(8,128)S(1)}, u32[]{:S(2)}, u32[]{:S(2)}) collective-permute-start(f32[64,16]{0,1:T(8,128)S(1)} %get-tuple-element.64), channel_id=1, source_target_pairs={{0,2},{2,0},{1,3},{3,1},{4,6},{6,4},{5,7},{7,5}} | collective-permute-start | bytes 12296 | tf_op jit(solution)/shard_map/ppermute | solution.py:611
  141.0 61.7 %copy-start.10 = (s32[256]{0:T(256)S(1)}, s32[256]{0:T(256)}, u32[]{:S(2)}) copy-start(s32[256]{0:T(256)} %copy-done.9) | copy-start | bytes 3076
  216.1 10.6 %collective-permute-start.3 = (f32[64,16]{0,1:T(8,128)S(1)}, f32[64,16]{0,1:T(8,128)S(1)}, u32[]{:S(2)}, u32[]{:S(2)}) collective-permute-start(f32[64,16]{0,1:T(8,128)S(1)} %get-tuple-element.61), channel_id=1, source_target_pairs={{0,2},{2,0},{1,3},{3,1},{4,6},{6,4},{5,7},{7,5}} | collective-permute-start | bytes 12296 | tf_op jit(solution)/shard_map/ppermute | solution.py:611
  218.3 2.8 copy-start.1
  220.4 1.3 copy-start.2
  221.7 3.1 %copy-start.8 = (s32[256]{0:T(256)S(1)}, s32[256]{0:T(256)}, u32[]{:S(2)}) copy-start(s32[256]{0:T(256)} %copy-done.7) | copy-start | bytes 3076
  227.0 2.2 copy-start.3

commit v2 on v1

v2 whole, which is shorter than its diff:
```python
import functools
import math
import jax
import jax.numpy as jnp
from jax import lax
from jax.experimental import pallas as pl
from jax.experimental.pallas import tpu as pltpu
from jax.sharding import PartitionSpec as P

EPSILON = 1e-6
ROPE_BASE = 50000.0
YARN_MSCALE = 1.0 + 0.1 * math.log(32.0)
MASK_VALUE = -1e30
GROUP = 8
RING = 4
AHEAD = 2
VIA_Y = 0
LANES = 128
PACK = 16
VMEM_BYTES = 67043328
VMEM_STEP = 1048576


def rope_tables(positions, rope_dim):
    half_dim = rope_dim // 2
    inv_freq = ROPE_BASE ** (-jnp.arange(half_dim).astype(jnp.float32) / half_dim)
    angles = positions.astype(jnp.float32)[:, None] * inv_freq[None, :]
    return jnp.cos(angles), jnp.sin(angles)


def insert_slot(i, start, pos_ref, latn_ref, ropen_ref, lat, rope):
    slots = lat.shape[0]
    rdim = rope.shape[0]
    s = pos_ref[i] - start
    inside = jnp.logical_and(s >= 0, s < slots)
    sc = jnp.where(inside, s, 0)
    r0 = pl.multiple_of((sc // PACK) * PACK, PACK)
    hit = lax.broadcasted_iota(jnp.int32, (PACK, 1), 0) == jnp.where(inside, sc - r0, -1)
    blk = lat[pl.ds(r0, PACK), :]
    lat[pl.ds(r0, PACK), :] = jnp.where(hit, latn_ref[pl.ds(i, 1), :], blk.astype(jnp.float32)).astype(jnp.bfloat16)
    c0 = pl.multiple_of((sc // LANES) * LANES, LANES)
    hit = lax.broadcasted_iota(jnp.int32, (1, LANES), 1) == jnp.where(inside, sc - c0, -1)
    eye = lax.broadcasted_iota(jnp.int32, (rdim, rdim), 0) == lax.broadcasted_iota(jnp.int32, (rdim, rdim), 1)
    col = jnp.sum(jnp.where(eye, ropen_ref[pl.ds(i, 1), :], 0.0), axis=1, keepdims=True)
    blk = rope[:, pl.ds(c0, LANES)]
    rope[:, pl.ds(c0, LANES)] = jnp.where(hit, col, blk.astype(jnp.float32)).astype(jnp.bfloat16)


def heads_kernel(cq_ref, cos_ref, sin_ref, wuq_ref, wuk_ref, qa_ref, qr_ref, wide, lines, rlines):
    block = wuq_ref.shape[0]
    nope = wuk_ref.shape[2]
    rank = wuk_ref.shape[0]
    rdim = wuq_ref.shape[1] - nope
    hdim = rdim // 2
    wide[...] = wuk_ref[...].astype(jnp.float32)
    cq = cq_ref[...]
    depth = cq.shape[1]
    dims = (((1,), (1,)), ((), ()))
    w_rope = wuq_ref[:, nope:, :].reshape(block * rdim, depth)
    r = lax.dot_general(cq, w_rope, dims, preferred_element_type=jnp.float32).astype(jnp.bfloat16).astype(jnp.float32)
    lane = lax.broadcasted_iota(jnp.int32, (1, block * rdim), 1)
    width = block * rdim
    turned = jnp.where(lane % rdim < hdim, -pltpu.roll(r, width - hdim, 1), pltpu.roll(r, hdim, 1))
    r = r * jnp.concatenate([cos_ref[...]] * block, axis=1) + turned * jnp.concatenate([sin_ref[...]] * block, axis=1)
    w_nope = wuq_ref[:, :nope, :].reshape(block * nope, depth)
    q = lax.dot_general(cq, w_nope, dims, preferred_element_type=jnp.float32).astype(jnp.bfloat16)
    for h in range(block):
        rlines[:, h, :rdim] = r[:, h * rdim:(h + 1) * rdim]
        wk = wide[:, h, :].astype(jnp.bfloat16)
        lines[:, h, :rank] = lax.dot_general(q[:, h * nope:(h + 1) * nope], wk, dims, preferred_element_type=jnp.float32)
    qa_ref[...] = lines[:, :, :rank].astype(jnp.bfloat16)
    qr_ref[...] = rlines[:, :, :rdim].astype(jnp.bfloat16)


def head_queries(cq, cos2, sin2, w_uq_t, w_uk):
    rows, qrank = cq.shape
    heads, qdim, _ = w_uq_t.shape
    rank, _, nope = w_uk.shape
    rdim = qdim - nope
    block = GROUP
    f32 = jnp.float32
    whole = lambda v: pl.BlockSpec(v.shape, lambda i: (0, 0))
    return pl.pallas_call(
        heads_kernel,
        grid=(heads // block,),
        in_specs=[
            whole(cq), whole(cos2), whole(sin2),
            pl.BlockSpec((block, qdim, qrank), lambda i: (i, 0, 0)),
            pl.BlockSpec((rank, block, nope), lambda i: (0, i, 0)),
        ],
        out_specs=[pl.BlockSpec((rows, block, d), lambda i: (0, i, 0)) for d in (rank, rdim)],
        out_shape=[jax.ShapeDtypeStruct((rows, heads, d), jnp.bfloat16) for d in (rank, rdim)],
        scratch_shapes=[
            pltpu.VMEM((rank, block, nope), f32),
            pltpu.VMEM((rows, block, rank + LANES), f32),
            pltpu.VMEM((rows, block, LANES), f32),
        ],
        compiler_params=pltpu.CompilerParams(dimension_semantics=('arbitrary',), vmem_limit_bytes=VMEM_BYTES - 8 * VMEM_STEP),
        cost_estimate=pl.CostEstimate(flops=2 * rows * heads * (qdim * qrank + nope * rank), bytes_accessed=2 * heads * (qdim * qrank + nope * rank), transcendentals=0),
        name='head_queries',
    )(cq, cos2, sin2, w_uq_t, w_uk)


def down_kernel(order_ref, hid_ref, wdq_ref, wkv_ref, gq_ref, gkv_ref, cos_ref, sin_ref, cq_ref, latn_ref, ropen_ref, pick, acc_q, acc_kv):
    i = pl.program_id(0)
    rows = hid_ref.shape[0]
    rank = gkv_ref.shape[0]
    hdim = cos_ref.shape[1] // 2

    @pl.when(i == 0)
    def _():
        pick[...] = (order_ref[...] == lax.broadcasted_iota(jnp.int32, (rows, rows), 1)).astype(jnp.bfloat16)
        acc_q[...] = jnp.zeros_like(acc_q)
        acc_kv[...] = jnp.zeros_like(acc_kv)

    x = jnp.dot(pick[...], hid_ref[...], preferred_element_type=jnp.float32).astype(jnp.bfloat16)
    acc_q[...] += jnp.dot(x, wdq_ref[...], preferred_element_type=jnp.float32)
    acc_kv[...] += lax.dot_general(x, wkv_ref[...], (((1,), (1,)), ((), ())), preferred_element_type=jnp.float32)

    @pl.when(i == pl.num_programs(0) - 1)
    def _():
        def normed(v, gain):
            v = v.astype(jnp.bfloat16).astype(jnp.float32)
            inv = lax.rsqrt(jnp.mean(v * v, axis=-1, keepdims=True) + EPSILON)
            return (v * inv * gain.astype(jnp.float32)[None, :]).astype(jnp.bfloat16)

        cq_ref[...] = normed(acc_q[...], gq_ref[...])
        latn_ref[...] = normed(acc_kv[:, :rank], gkv_ref[...]).astype(jnp.float32)
        r = acc_kv[:, rank:].astype(jnp.bfloat16).astype(jnp.float32)
        turned = jnp.concatenate([-r[:, hdim:], r[:, :hdim]], axis=1)
        ropen_ref[...] = (r * cos_ref[...] + turned * sin_ref[...]).astype(jnp.bfloat16).astype(jnp.float32)


def down_project(order, hidden, w_dq, w_dkv_t, gain_q, gain_kv, cos2, sin2):
    rows, dmodel = hidden.shape
    qrank = w_dq.shape[1]
    width = w_dkv_t.shape[0]
    rank = gain_kv.shape[0]
    block = 1024
    fixed = lambda i: (0, 0)
    return pl.pallas_call(
        down_kernel,
        grid=(dmodel // block,),
        in_specs=[
            pl.BlockSpec((rows, 1), fixed),
            pl.BlockSpec((rows, block), lambda i: (0, i)),
            pl.BlockSpec((block, qrank), lambda i: (i, 0)),
            pl.BlockSpec((width, block), lambda i: (0, i)),
            pl.BlockSpec((qrank,), lambda i: (0,)),
            pl.BlockSpec((rank,), lambda i: (0,)),
            pl.BlockSpec(cos2.shape, fixed),
            pl.BlockSpec(sin2.shape, fixed),
        ],
        out_specs=[pl.BlockSpec((rows, qrank), fixed), pl.BlockSpec((rows, rank), fixed), pl.BlockSpec((rows, width - rank), fixed)],
        out_shape=[
            jax.ShapeDtypeStruct((rows, qrank), jnp.bfloat16),
            jax.ShapeDtypeStruct((rows, rank), jnp.float32),
            jax.ShapeDtypeStruct((rows, width - rank), jnp.float32),
        ],
        scratch_shapes=[
            pltpu.VMEM((rows, rows), jnp.bfloat16),
            pltpu.VMEM((rows, qrank), jnp.float32),
            pltpu.VMEM((rows, width), jnp.float32),
        ],
        compiler_params=pltpu.CompilerParams(dimension_semantics=('arbitrary',), vmem_limit_bytes=VMEM_BYTES - 8 * VMEM_STEP),
        cost_estimate=pl.CostEstimate(flops=2 * rows * dmodel * (qrank + width + rows), bytes_accessed=2 * dmodel * (qrank + width), transcendentals=0),
        name='down_project',
    )(order[:, None], hidden, w_dq, w_dkv_t, gain_q, gain_kv, cos2, sin2)


def attend_kernel(first, steps, scale, order_ref, pos_ref, where_ref, qa_ref, qr_ref, latn_ref, ropen_ref, lat_hbm, rope_hbm, *rest):
    uo_ref, us_ref, mo_ref, lo_ref, ms_ref, ls_ref, lat_out, rope_out, lat_buf, rope_buf, in_sem, out_sem = rest[-12:]
    t = pl.program_id(0)
    slots = lat_buf.shape[2]
    heads = qa_ref.shape[1]
    half = heads // 2
    start = where_ref[0]
    own = where_ref[1]

    def reads(step):
        ring = lax.rem(step, RING)
        out = []
        for g in range(GROUP):
            b = order_ref[first + step * GROUP + g]
            out.append(pltpu.make_async_copy(lat_hbm.at[b], lat_buf.at[ring, g], in_sem.at[ring, g, 0]))
            out.append(pltpu.make_async_copy(rope_hbm.at[b], rope_buf.at[ring, g], in_sem.at[ring, g, 1]))
        return out

    def writes(step):
        ring = lax.rem(step, RING)
        out = []
        for g in range(GROUP):
            b = order_ref[first + step * GROUP + g]
            out.append(pltpu.make_async_copy(lat_buf.at[ring, g], lat_out.at[b], out_sem.at[ring, g, 0]))
            out.append(pltpu.make_async_copy(rope_buf.at[ring, g], rope_out.at[b], out_sem.at[ring, g, 1]))
        return out

    @pl.when(t == 0)
    def _():
        for s in range(min(AHEAD, steps)):
            for c in reads(s):
                c.start()

    lag = RING - AHEAD

    @pl.when(t >= lag)
    def _():
        for c in writes(t - lag):
            c.wait()

    @pl.when(t + AHEAD < steps)
    def _():
        for c in reads(t + AHEAD):
            c.start()

    for c in reads(t):
        c.wait()

    ring = lax.rem(t, RING)
    lanes = lax.broadcasted_iota(jnp.int32, (1, LANES), 1)
    for g in range(GROUP):
        insert_slot(first + t * GROUP + g, start, pos_ref, latn_ref, ropen_ref, lat_buf.at[ring, g], rope_buf.at[ring, g])

    slot_ids = lax.broadcasted_iota(jnp.int32, (1, slots), 1) + start
    o0 = pl.multiple_of(own * half, half)
    o1 = pl.multiple_of((1 - own) * half, half)
    scores = []
    for g in range(GROUP):
        i = first + t * GROUP + g
        qa = jnp.concatenate([qa_ref[g, pl.ds(o0, half), :], qa_ref[g, pl.ds(o1, half), :]], axis=0)
        qr = jnp.concatenate([qr_ref[g, pl.ds(o0, half), :], qr_ref[g, pl.ds(o1, half), :]], axis=0)
        s = lax.dot_general(qa, lat_buf[ring, g], (((1,), (1,)), ((), ())), preferred_element_type=jnp.float32)
        s = (s + jnp.dot(qr, rope_buf[ring, g], preferred_element_type=jnp.float32)) * scale
        scores.append(jnp.where(slot_ids <= pos_ref[i], s, MASK_VALUE))
    ms = jnp.concatenate([mo_ref[...], ms_ref[...]], axis=0)
    ls = jnp.concatenate([lo_ref[...], ls_ref[...]], axis=0)
    for g in range(GROUP):
        i = first + t * GROUP + g
        m = jnp.max(scores[g], axis=1, keepdims=True)
        p = jnp.where(slot_ids <= pos_ref[i], jnp.exp(scores[g] - m), 0.0)
        l = jnp.sum(p, axis=1, keepdims=True)
        u = jnp.dot(p.astype(jnp.bfloat16), lat_buf[ring, g], preferred_element_type=jnp.float32)
        uo_ref[g] = u[:half]
        us_ref[g] = u[half:]
        j = t * GROUP + g
        ms = jnp.where(lanes == j, m, ms)
        ls = jnp.where(lanes == j, l, ls)
    mo_ref[...] = ms[:half]
    lo_ref[...] = ls[:half]
    ms_ref[...] = ms[half:]
    ls_ref[...] = ls[half:]

    for c in writes(t):
        c.start()

    @pl.when(t == steps - 1)
    def _():
        for s in range(max(0, steps - lag), steps):
            for c in writes(s):
                c.wait()


def attend_chunk(first, count, scale, order, pos, where, qa, qr, latn, ropen, lat, rope, prev):
    steps = count // GROUP
    heads, rank = qa.shape[1:]
    rdim = qr.shape[2]
    slots = lat.shape[1]
    half = heads // 2
    base = first // GROUP
    any_spec = pl.BlockSpec(memory_space=pl.ANY)
    fixed = lambda t, *_: (0, 0)
    bf16, f32 = jnp.bfloat16, jnp.float32
    dma = pltpu.SemaphoreType.DMA((RING, GROUP, 2))
    part = jax.ShapeDtypeStruct((count, half, rank), f32)
    tile = jax.ShapeDtypeStruct((half, LANES), f32)
    return pl.pallas_call(
        functools.partial(attend_kernel, first, steps, scale),
        grid_spec=pltpu.PrefetchScalarGridSpec(
            num_scalar_prefetch=3,
            grid=(steps,),
            in_specs=[pl.BlockSpec((GROUP, heads, d), lambda t, *_: (base + t, 0, 0)) for d in (rank, rdim)]
            + [pl.BlockSpec(v.shape, fixed) for v in (latn, ropen)] + [any_spec] * (2 + len(prev)),
            out_specs=[pl.BlockSpec((GROUP, half, rank), lambda t, *_: (t, 0, 0))] * 2 + [pl.BlockSpec(tile.shape, fixed)] * 4 + [any_spec] * 2,
            scratch_shapes=[
                pltpu.VMEM((RING, GROUP, slots, rank), bf16),
                pltpu.VMEM((RING, GROUP, rdim, slots), bf16),
                dma, dma,
            ],
        ),
        out_shape=[part] * 2 + [tile] * 4 + [jax.ShapeDtypeStruct(v.shape, bf16) for v in (lat, rope)],
        input_output_aliases={9: 6, 10: 7} if prev else {},
        compiler_params=pltpu.CompilerParams(dimension_semantics=('arbitrary',), vmem_limit_bytes=VMEM_BYTES - 8 * VMEM_STEP),
        cost_estimate=pl.CostEstimate(
            flops=64 * count * heads * slots * rank, bytes_accessed=count * slots * (rank + rdim) * 4, transcendentals=0),
        name='attend_chunk_%d' % first,
    )(order, pos, where, qa, qr, latn, ropen, lat, rope, *prev)


def finish_kernel(place_ref, mk_ref, lk_ref, m0_ref, l0_ref, m1_ref, l1_ref, uk_hbm, ux_hbm, uo_hbm, us_hbm, wvh_hbm, hid_hbm, w_hbm, out_hbm, wbuf, part, got_c, sum_c, got_t, full, staged, o_got, o1, o2, ua, ux, ub, ud, un, wv_heads, mg, lg, hid, outv, w_sem, o_sem, c_sem, t_sem, ay_sem, ax_sem, af_sem, ac_sem, a_sem, b_sem, d_sem, ml_sem, v_sem, h_sem, r_sem):
    blocks, rows, width = part.shape
    half_blocks = blocks // 2
    r2, r4 = rows // 2, rows // 4
    depth = wbuf.shape[1]
    sp = lax.axis_index('sp')
    tp = lax.axis_index('tp')
    core = lax.rem(sp, 2)
    xpos = sp // 2
    sib = {'sp': sp + 1 - 2 * core}
    nbx = {'sp': lax.rem(sp + 2, 4)}
    nby = {'tp': 1 - tp}
    mesh_id = pl.DeviceIdType.MESH

    def remote(src, dst, sems, j, to, k=0):
        return pltpu.make_async_remote_copy(src_ref=src, dst_ref=dst, send_sem=sems.at[0, k, j], recv_sem=sems.at[1, k, j], device_id=to, device_id_type=mesh_id)

    def wcopy(j):
        col = lax.rem(j, half_blocks)
        return pltpu.make_async_copy(
            w_hbm.at[pl.ds(pl.multiple_of(core * depth, depth), depth), pl.ds(pl.multiple_of(col * width, width), width)],
            wbuf.at[lax.rem(j, wbuf.shape[0])], w_sem.at[lax.rem(j, wbuf.shape[0])])

    def spot(j, x, c, t):
        first = pl.multiple_of((j // half_blocks) * 4 * rows // 2 + ((x * 2 + c) * 2 + t) * r4, r4)
        return full.at[lax.rem(j, half_blocks), pl.ds(first, r4)]

    def send_o():
        return remote(o2.at[pl.ds(rows, rows)], o_got, o_sem, 0, nbx)

    def copy_c(j):
        return remote(part.at[j, pl.ds(pl.multiple_of((1 - core) * r2, r2), r2)], got_c.at[j], c_sem, j, sib)

    def copy_t(j):
        return remote(sum_c.at[j, pl.ds(pl.multiple_of((1 - tp) * r4, r4), r4)], got_t.at[j], t_sem, j, nby)

    def copy_ay(j):
        return remote(spot(j, xpos, core, tp), spot(j, xpos, core, tp), ay_sem, j, nby)

    def copy_ax(j):
        return remote(spot(j, xpos, core, tp), spot(j, xpos, core, tp), ax_sem, j, nbx)

    def copy_af(j):
        return remote(spot(j, xpos, core, 1 - tp), spot(j, xpos, core, 1 - tp), af_sem, j, nbx)

    def copy_ag(j):
        return remote(spot(j, 1 - xpos, core, tp), spot(j, 1 - xpos, core, tp), af_sem, j, nby)

    via_y = VIA_Y

    def emit_out(cb):
        cols = pl.ds(pl.multiple_of(cb * width, width), width)
        return pltpu.make_async_copy(outv.at[:, cols], out_hbm.at[:, cols], r_sem.at[cb])

    def copy_ac(j, k):
        x = xpos if k < 2 else 1 - xpos
        t = tp if k % 2 == 0 else 1 - tp
        return remote(spot(j, x, core, t), spot(j, x, core, t), ac_sem, j, sib, k)

    half = uk_hbm.shape[1]
    vdim = wvh_hbm.shape[2]
    quad = half // 2
    steps_b = ud.shape[0]
    rows_b = ud.shape[1]
    side_b = steps_b // 2

    def mine_a(k):
        if k == 0:
            return pltpu.make_async_copy(uk_hbm, ua, a_sem.at[0])
        return pltpu.make_async_copy(ux_hbm, ux, a_sem.at[1])

    def mine_b(k):
        return pltpu.make_async_copy(uo_hbm.at[pl.ds(k * rows_b, rows_b)], ub.at[k], b_sem.at[k])

    def theirs_b(k):
        return remote(us_hbm.at[pl.ds(k * rows_b, rows_b)], ud.at[k], d_sem, k, sib)

    get_wv = pltpu.make_async_copy(wvh_hbm, wv_heads, v_sem)
    get_hid = pltpu.make_async_copy(hid_hbm, hid, h_sem)
    order_b = list(range(side_b, steps_b)) + list(range(side_b))
    for k in range(2):
        mine_a(k).start()
    get_wv.start()
    for j in range(wbuf.shape[0] - 1):
        wcopy(j).start()
    for k in order_b:
        mine_b(k).start()
    get_hid.start()
    barrier = pltpu.get_barrier_semaphore()
    for to in (sib, nbx, nby):
        pl.semaphore_signal(barrier, inc=1, device_id=to, device_id_type=mesh_id)
    pl.semaphore_wait(barrier, 3)
    tiles = [remote(src, dst, ml_sem, k, sib) for k, (src, dst) in enumerate(((m1_ref, mg), (l1_ref, lg)))]
    for c in tiles:
        c.start()
    for k in order_b:
        theirs_b(k).start()

    lanes = lax.broadcasted_iota(jnp.int32, (1, 128), 1)

    def weights(m0, l0, m1, l1):
        m = jnp.maximum(m0, m1)
        a0 = jnp.exp(m0 - m)
        a1 = jnp.exp(m1 - m)
        l = l0 * a0 + l1 * a1
        inv = 1.0 / jnp.where(l > 0, l, 1.0)
        return a0 * inv, a1 * inv

    def merge_row(w, lane, first, second, to):
        hit = lanes == lane
        c0 = jnp.sum(jnp.where(hit, w[0], 0.0), axis=1, keepdims=True)
        c1 = jnp.sum(jnp.where(hit, w[1], 0.0), axis=1, keepdims=True)
        u = first * c0 + second * c1
        un[0, to, :, :u.shape[1]] = u[:quad]
        un[1, to, :, :u.shape[1]] = u[quad:]

    rank = uk_hbm.shape[2]

    def heads_out(to, first):
        def one(h, carry):
            for p in range(2):
                u = un[p, :, h, :rank].astype(jnp.bfloat16)
                o = jnp.dot(u, wv_heads[p * quad + h], preferred_element_type=jnp.float32)
                to[pl.ds(first, rows), pl.ds(pl.multiple_of((p * quad + h) * vdim, vdim), vdim)] = o.astype(to.dtype)
            return carry
        for h in range(quad):
            one(h, 0)

    def rows_of(k, q):
        mine_b(k).wait()
        theirs_b(k).wait_recv()
        w = weights(m0_ref[...], l0_ref[...], mg[...], lg[...])
        for e in range(rows_b):
            merge_row(w, k * rows_b + e, ub[k, e], ud[k, e], pl.multiple_of(q * rows_b, rows_b) + e)

    def first_side(q, carry):
        rows_of(side_b + q, q)
        return carry

    for k in range(2):
        mine_a(k).wait()
    wa = weights(mk_ref[...], lk_ref[...], ux[rows, :, :128], ux[rows, :, 128:256])

    def rows_a(q, carry):
        for e in range(8):
            r = q * 8 + e
            merge_row(wa, xpos * rows + r, ua[r], ux[r], r)
        return carry

    lax.fori_loop(0, rows // 8, rows_a, 0)
    get_wv.wait()
    heads_out(o1, 0)
    for c in tiles:
        c.wait()

    def second_group(i):
        per = side_b // 2

        @pl.when(i == 1)
        def _():
            lax.fori_loop(0, side_b, first_side, 0)
            heads_out(o2, rows)

            @pl.when(xpos == 0)
            def _():
                send_o().start()

        @pl.when(jnp.logical_and(i >= 3, i < 5))
        def _():
            def one(e, carry):
                q = (i - 3) * per + e
                rows_of(q, q)
                return carry

            lax.fori_loop(0, per, one, 0)

        @pl.when(i == 4)
        def _():
            heads_out(o2, 0)

    def body(i, carry):
        j = i

        @pl.when(j < blocks)
        def _():
            @pl.when(jnp.logical_and(j == half_blocks, xpos == 1))
            def _():
                send_o().wait_recv()

            wcopy(j).wait()
            w = wbuf.at[lax.rem(j, wbuf.shape[0])]

            @pl.when(j < half_blocks)
            def _():
                part[j] = jnp.dot(o1[...], w[...], preferred_element_type=jnp.float32)

            @pl.when(j >= half_blocks)
            def _():
                o = jnp.where(xpos == 0, o2[pl.ds(0, rows)], o_got[...])
                part[j] = jnp.dot(o.astype(jnp.bfloat16), w[...], preferred_element_type=jnp.float32)

            @pl.when(j + wbuf.shape[0] - 1 < blocks)
            def _():
                wcopy(j + wbuf.shape[0] - 1).start()

            copy_c(j).start()

        j1 = i - 1

        @pl.when(jnp.logical_and(j1 >= 0, j1 < blocks))
        def _():
            copy_c(j1).wait_recv()
            sum_c[j1] = part[j1, pl.ds(pl.multiple_of(core * r2, r2), r2)] + got_c[j1]
            copy_t(j1).start()

        second_group(i)

        j2 = i - 3

        @pl.when(jnp.logical_and(j2 >= 0, j2 < blocks))
        def _():
            copy_t(j2).wait_recv()
            first = pl.multiple_of((j2 // half_blocks) * 2 * rows + ((xpos * 2 + core) * 2 + tp) * r4, r4)
            full[lax.rem(j2, half_blocks), pl.ds(first, r4)] = sum_c[j2, pl.ds(pl.multiple_of(tp * r4, r4), r4)] + got_t[j2]
            copy_ay(j2).start()
            copy_ax(j2).start()
            copy_ac(j2, 0).start()

        j3 = i - 5

        @pl.when(jnp.logical_and(j3 >= 0, j3 < blocks))
        def _():
            copy_ay(j3).wait_recv()

            @pl.when(j3 >= via_y)
            def _():
                copy_af(j3).start()

            copy_ac(j3, 1).start()
            copy_ax(j3).wait_recv()

            @pl.when(j3 < via_y)
            def _():
                copy_ag(j3).start()

            copy_ac(j3, 2).start()

        j4 = i - 7

        @pl.when(jnp.logical_and(j4 >= 0, j4 < blocks))
        def _():
            copy_af(j4).wait_recv()
            copy_ac(j4, 3).start()

        j5 = i - 8

        @pl.when(jnp.logical_and(j5 >= 0, j5 < blocks))
        def _():
            for k in range(4):
                copy_ac(j5, k).wait_recv()

        @pl.when(jnp.logical_and(j5 >= half_blocks, j5 < blocks))
        def _():
            cb = j5 - half_blocks
            cols = pl.ds(pl.multiple_of(cb * width, width), width)
            staged[...] = full[cb]

            @pl.when(cb == 0)
            def _():
                get_hid.wait()


            def emit(q, carry):
                b = pl.multiple_of(q * 16, 16)
                lines = [staged[pl.ds(place_ref[b + r], 1), :] for r in range(16)]
                y = jnp.concatenate(lines, axis=0)
                outv[pl.ds(b, 16), cols] = (hid[pl.ds(b, 16), cols].astype(jnp.float32) + y).astype(jnp.bfloat16)
                return carry

            lax.fori_loop(0, outv.shape[0] // 16, emit, 0)
            emit_out(cb).start()

        return carry

    lax.fori_loop(0, blocks + 8, body, 0)

    def drain(j, carry):
        copy_c(j).wait_send()
        copy_t(j).wait_send()
        copy_ay(j).wait_send()
        copy_ax(j).wait_send()
        copy_af(j).wait_send()
        for k in range(4):
            copy_ac(j, k).wait_send()
        return carry

    lax.fori_loop(0, blocks, drain, 0)
    for k in range(steps_b):
        theirs_b(k).wait_send()
    for k in range(half_blocks):
        emit_out(k).wait()

    @pl.when(xpos == 0)
    def _():
        send_o().wait_send()


def finish(place, first, second, hidden, wv_heads, w_out, blocks, tag):
    mk, lk, uk, ux = first
    m0, l0, m1, l1, uo, us = second
    rows, half, rank = uk.shape
    vdim = wv_heads.shape[2]
    depth = half * vdim
    batch, dmodel = hidden.shape
    width = dmodel // (blocks // 2)
    vmem = pl.BlockSpec(memory_space=pltpu.VMEM)
    any_spec = pl.BlockSpec(memory_space=pl.ANY)
    ring = 2
    rows_b = 8
    steps_b = 2 * rows // rows_b
    f32 = jnp.float32
    return pl.pallas_call(
        finish_kernel,
        in_specs=[pl.BlockSpec(memory_space=pltpu.SMEM)] + [vmem] * 6 + [any_spec] * 7,
        out_specs=any_spec,
        out_shape=jax.ShapeDtypeStruct((batch, dmodel), jnp.bfloat16),
        scratch_shapes=[
            pltpu.VMEM((ring, depth, width), jnp.bfloat16),
            pltpu.VMEM((blocks, rows, width), f32),
            *[pltpu.VMEM((blocks, rows // 2, width), f32)] * 2,
            pltpu.VMEM((blocks, rows // 4, width), f32),
            pltpu.VMEM((blocks // 2, batch, width), f32),
            pltpu.VMEM((batch, width), f32),
            pltpu.VMEM((rows, depth), f32),
            pltpu.VMEM((rows, depth), jnp.bfloat16),
            pltpu.VMEM((2 * rows, depth), f32),
            pltpu.VMEM((rows, half, rank), f32),
            pltpu.VMEM((rows + 1, half, rank), f32),
            pltpu.VMEM((steps_b, rows_b, half, rank), f32),
            pltpu.VMEM((steps_b, rows_b, half, rank), f32),
            pltpu.VMEM((2, rows, half // 2, rank + 128), f32),
            pltpu.VMEM((half, rank, vdim), jnp.bfloat16),
            pltpu.VMEM((half, LANES), f32),
            pltpu.VMEM((half, LANES), f32),
            pltpu.VMEM((batch, dmodel), jnp.bfloat16),
            pltpu.VMEM((batch, dmodel), jnp.bfloat16),
            pltpu.SemaphoreType.DMA((ring,)),
            pltpu.SemaphoreType.DMA((2, 1, 1)),
            *[pltpu.SemaphoreType.DMA((2, 1, blocks))] * 5,
            pltpu.SemaphoreType.DMA((2, 4, blocks)),
            pltpu.SemaphoreType.DMA((2,)),
            pltpu.SemaphoreType.DMA((steps_b,)),
            pltpu.SemaphoreType.DMA((2, 1, steps_b)),
            pltpu.SemaphoreType.DMA((2, 1, 2)),
            pltpu.SemaphoreType.DMA,
            pltpu.SemaphoreType.DMA,
            pltpu.SemaphoreType.DMA((blocks // 2,)),
        ],
        compiler_params=pltpu.CompilerParams(collective_id=tag, has_side_effects=True, vmem_limit_bytes=VMEM_BYTES),
        name='finish_%d' % tag,
    )(place, mk, lk, m0, l0, m1, l1, uk, ux, uo, us, wv_heads, hidden, w_out)


def pair_kernel(m0_ref, l0_ref, m1_ref, l1_ref, uo_hbm, us_hbm, wuv_hbm, keep_ref, send_ref, m_ref, l_ref, wvh_ref, got, own, mg, lg, wv, wv_wide, ml_sem, d_sem, o_sem, v_sem):
    blocks, rows = own.shape[0], own.shape[1]
    sp = lax.axis_index('sp')
    xpos = sp // 2
    sib = {'sp': sp + 1 - 2 * lax.rem(sp, 2)}
    mesh_id = pl.DeviceIdType.MESH

    def remote(src, dst, sems, j):
        return pltpu.make_async_remote_copy(src_ref=src, dst_ref=dst, send_sem=sems.at[0, j], recv_sem=sems.at[1, j], device_id=sib, device_id_type=mesh_id)

    def mine(j):
        return pltpu.make_async_copy(uo_hbm.at[pl.ds(j * rows, rows)], own.at[j], o_sem.at[j])

    def theirs(j):
        return remote(us_hbm.at[pl.ds(j * rows, rows)], got.at[j], d_sem, j)

    half = uo_hbm.shape[1]
    quad = half // 2
    core = lax.rem(sp, 2)
    get_wv = pltpu.make_async_copy(wuv_hbm.at[:, pl.ds(pl.multiple_of(core * half, half), half)], wv, v_sem)
    get_wv.start()
    barrier = pltpu.get_barrier_semaphore()
    pl.semaphore_signal(barrier, inc=1, device_id=sib, device_id_type=mesh_id)
    for j in range(blocks):
        mine(j).start()
    pl.semaphore_wait(barrier, 1)
    cm = remote(m1_ref, mg, ml_sem, 0)
    cl = remote(l1_ref, lg, ml_sem, 1)
    cm.start()
    cl.start()
    for j in range(blocks):
        theirs(j).start()
    get_wv.wait()
    for p in range(2):
        wv_wide[...] = wv[:, p * quad:(p + 1) * quad, :].astype(jnp.float32)
        for h in range(quad):
            wvh_ref[p * quad + h] = wv_wide[:, h, :].astype(jnp.bfloat16)
    cm.wait()
    cl.wait()
    m0, m1 = m0_ref[...], mg[...]
    m = jnp.maximum(m0, m1)
    a0 = jnp.exp(m0 - m)
    a1 = jnp.exp(m1 - m)
    m_ref[...] = m
    l = l0_ref[...] * a0 + lg[...] * a1
    l_ref[...] = l
    send_ref[blocks * rows // 2] = jnp.concatenate([m, l, m, l], axis=1)
    lanes = lax.broadcasted_iota(jnp.int32, (1, 128), 1)

    def merge_block(j, out_ref, first):
        mine(j).wait()
        theirs(j).wait_recv()
        for r in range(rows):
            hit = lanes == j * rows + r
            c0 = jnp.sum(jnp.where(hit, a0, 0.0), axis=1, keepdims=True)
            c1 = jnp.sum(jnp.where(hit, a1, 0.0), axis=1, keepdims=True)
            out_ref[first + r] = own[j, r] * c0 + got[j, r] * c1

    side = blocks // 2

    def body(j, carry):
        merge_block((1 - xpos) * side + j, send_ref, j * rows)
        merge_block(xpos * side + j, keep_ref, j * rows)
        return carry

    lax.fori_loop(0, side, body, 0)

    def drain(j, carry):
        theirs(j).wait_send()
        return carry

    lax.fori_loop(0, blocks, drain, 0)


def pair_merge(mo, lo, ms, ls, uo, us, w_uv, tag):
    count, half, rank = uo.shape
    vdim = w_uv.shape[2]
    rows = 8
    blocks = count // rows
    vmem = pl.BlockSpec(memory_space=pltpu.VMEM)
    any_spec = pl.BlockSpec(memory_space=pl.ANY)
    return pl.pallas_call(
        pair_kernel,
        in_specs=[vmem, vmem, vmem, vmem, any_spec, any_spec, any_spec],
        out_specs=[vmem, vmem, vmem, vmem, vmem],
        out_shape=[
            jax.ShapeDtypeStruct((count // 2, half, rank), jnp.float32),
            jax.ShapeDtypeStruct((count // 2 + 1, half, rank), jnp.float32),
            jax.ShapeDtypeStruct((half, LANES), jnp.float32),
            jax.ShapeDtypeStruct((half, LANES), jnp.float32),
            jax.ShapeDtypeStruct((half, rank, vdim), jnp.bfloat16),
        ],
        scratch_shapes=[
            pltpu.VMEM((blocks, rows, half, rank), jnp.float32),
            pltpu.VMEM((blocks, rows, half, rank), jnp.float32),
            pltpu.VMEM((half, LANES), jnp.float32),
            pltpu.VMEM((half, LANES), jnp.float32),
            pltpu.VMEM((rank, half, vdim), jnp.bfloat16),
            pltpu.VMEM((rank, half // 2, vdim), jnp.float32),
            pltpu.SemaphoreType.DMA((2, 2)),
            pltpu.SemaphoreType.DMA((2, blocks)),
            pltpu.SemaphoreType.DMA((blocks,)),
            pltpu.SemaphoreType.DMA,
        ],
        compiler_params=pltpu.CompilerParams(collective_id=tag, has_side_effects=True, vmem_limit_bytes=VMEM_BYTES - 4 * VMEM_STEP),
        name='pair_merge_%d' % tag,
    )(mo, lo, ms, ls, uo, us, w_uv)


def merge_tiles(m0, l0, u0, m1, l1, u1):
    m = jnp.maximum(m0, m1)
    a0 = jnp.exp(m0 - m)
    a1 = jnp.exp(m1 - m)
    count = u0.shape[0]
    return m, l0 * a0 + l1 * a1, u0 * a0[:, :count].T[:, :, None] + u1 * a1[:, :count].T[:, :, None]


def solution(mesh):
    row_spec = P('dp', None)
    cache_spec = P('dp', 'sp', None)
    head_spec = P(None, 'tp', None)
    in_specs = (row_spec, cache_spec, cache_spec, P('dp'), P(), P(), P(), P(), head_spec, head_spec, head_spec, P('tp', None))
    out_specs = (row_spec, cache_spec, cache_spec)
    sibling = [(0, 1), (1, 0), (2, 3), (3, 2)]
    across = [(0, 2), (2, 0), (1, 3), (3, 1)]

    def local_step(hidden, lat_cache, rope_cache, positions, w_dq, gain_q, w_dkv, gain_kv, w_uq, w_uk, w_uv, w_out):
        rows = hidden.shape[0]
        slots = lat_cache.shape[1]
        heads = w_uq.shape[1]
        half = heads // 2
        scale = YARN_MSCALE ** 2 / math.sqrt(w_uq.shape[2])
        sp = lax.axis_index('sp')
        core = sp % 2
        xpos = sp // 2
        ids = jnp.arange(rows, dtype=jnp.int32)
        ahead = (positions[None, :] > positions[:, None]) | ((positions[None, :] == positions[:, None]) & (ids[None, :] < ids[:, None]))
        rank_of = jnp.sum(ahead.astype(jnp.int32), axis=1)
        pick = rank_of[None, :] == ids[:, None]
        order = jnp.sum(jnp.where(pick, ids[None, :], 0), axis=1)
        pos = jnp.sum(jnp.where(pick, positions[None, :], 0), axis=1)
        cos_t, sin_t = rope_tables(pos, rope_cache.shape[2])
        cos2 = jnp.concatenate([cos_t, cos_t], axis=1)
        sin2 = jnp.concatenate([sin_t, sin_t], axis=1)
        cq, latn, ropen = down_project(order, hidden, w_dq, jnp.transpose(w_dkv), gain_q, gain_kv, cos2, sin2)
        rope_t = jnp.swapaxes(rope_cache, 1, 2)
        where = jnp.stack([sp * slots, core]).astype(jnp.int32)
        q_abs, q_rope = head_queries(cq, cos2, sin2, jnp.transpose(w_uq, (1, 2, 0)), w_uk)

        half_rows = rows // 2
        own_rows = rows // 4
        args = (scale, order, pos)
        uo, us, mo, lo, ms, ls, *held = attend_chunk(0, half_rows, *args, where, q_abs, q_rope, latn, ropen, lat_cache, rope_t, [])
        keep, send, mk, lk, wv_heads = pair_merge(mo, lo, ms, ls, uo, us, w_uv, 2)
        where, send = lax.optimization_barrier((where, send))
        ux = lax.ppermute(send, 'sp', across)
        uo, us, mo, lo, ms, ls, lat_out, rope_n = attend_chunk(half_rows, half_rows, *args, where, q_abs, q_rope, latn, ropen, lat_cache, rope_t, held)
        rope_out = jnp.swapaxes(rope_n, 1, 2)
        r = rank_of % half_rows
        x, k = r // own_rows, r % own_rows
        quarter = own_rows // 4
        c, t = k // (2 * quarter), (k // quarter) % 2
        place = (rank_of // half_rows) * half_rows + ((x * 2 + c) * 2 + t) * quarter + k % quarter
        place = place.astype(jnp.int32)

        def far(_, second):
            m0, l0, m1, l1, u0, u1 = second
            gm0, gl0, gm1, gl1, gu0, gu1 = lax.ppermute(second, 'sp', across)
            m0, l0, u0 = merge_tiles(m0, l0, u0, gm0, gl0, gu0)
            m1, l1, u1 = merge_tiles(m1, l1, u1, gm1, gl1, gu1)
            return m0, l0, m1, l1, u0, u1

        trips = (pos[half_rows] >= 2 * slots).astype(jnp.int32)
        ux, uo = lax.optimization_barrier((ux, uo))
        second = lax.fori_loop(0, trips, far, (mo, lo, ms, ls, uo, us))
        out = finish(place, (mk, lk, keep, ux), second, hidden, wv_heads, w_out, 12, 3)
        return out, lat_out, rope_out

    return jax.shard_map(local_step, mesh=mesh, in_specs=in_specs, out_specs=out_specs, check_vma=False)
```

time: 293 us -> 253 us (0.86)
  matrix products: 24 us -> 0 us
  local copies, waits for them, and re-layouts: 23.3 us -> 5.76 us
  Pallas kernels: 228 us -> 237 us
  other arithmetic: 9.38 us -> 4.4 us
    dot_general x5 -> x0, matrix products: 24 us -> none  [the longest x1 10.5 us: project_inputs(): jnp.dot(hidden, w_dq, preferred_element_type=jnp.float32)]
    pallas_call x1 -> x2, Pallas kernels: 30.3 us -> 41.9 us  [the longest x1 25.6 us: head_queries(): pl.pallas_call(heads_kernel, grid=(heads // block,), in_specs=[whole(cq),...]
    pallas_call x1, Pallas kernels: 55.8 us -> 67 us  [finish(): pl.pallas_call(finish_kernel, in_specs=[pl.BlockSpec(memory_space=pltpu.S...]
    pallas_call x2 -> x1, Pallas kernels: 21.6 us -> 13 us  [pair_merge(): pl.pallas_call(pair_kernel, in_specs=[vmem, vmem, vmem, vmem, any_spec, a...]
    dynamic_slice x4 -> x0, local copies, waits for them, and re-layouts: 8.03 us -> none  [the longest x3 5.92 us: local_step(): lax.dynamic_slice_in_dim(v, (1 - xpos) * own_rows, own_rows, 0)]
    convert_element_type x8 -> x0, other arithmetic: 5.45 us -> none  [the longest x1 2.22 us: local_step(): lat1 = (u1 / l1[:, :, None]).astype(jnp.bfloat16)]
    slice x5 -> x1, local copies, waits for them, and re-layouts: 5.86 us -> 0.51 us  [local_step(): trips = (pos[half_rows] >= 2 * slots).astype(jnp.int32)]
    pallas_call x2, Pallas kernels: 120 us -> 116 us  [attend_chunk(): pl.pallas_call(functools.partial(attend_kernel, first, steps, scale), gri...]
  transfers between devices with their start and end apart: 3 -> 1, of which waited for: 0 -> 0; matrix products, arithmetic and copies ran while one was open for 4% -> 0% of each run, Pallas kernels for 24% -> 23%
where the time goes in v2:
time: 253 us; the launch traced here: 252 us
  Pallas kernels  237 us (94%)
  local copies, waits for them, and re-layouts  5.76 us (2%)
  other arithmetic  4.4 us (2%)
  starting transfers between devices  3.15 us (1%)
    pallas_call x2, Pallas kernels, attend_chunk(): pl.pallas_call(functools.partial(attend_kernel, first, steps, scale), gri...  116 us
    pallas_call x1, Pallas kernels, finish(): pl.pallas_call(finish_kernel, in_specs=[pl.BlockSpec(memory_space=pltpu.S...  67 us
    pallas_call x1, Pallas kernels, head_queries(): pl.pallas_call(heads_kernel, grid=(heads // block,), in_specs=[whole(cq),...  25.6 us
    pallas_call x1, Pallas kernels, down_project(): pl.pallas_call(down_kernel, grid=(dmodel // block,), in_specs=[pl.BlockSp...  16.3 us
    pallas_call x1, Pallas kernels, pair_merge(): pl.pallas_call(pair_kernel, in_specs=[vmem, vmem, vmem, vmem, any_spec, a...  13 us
  transfers between devices with their start and end apart: 1, of which 0 were waited for; matrix products, arithmetic and copies ran while one was open for 0% of the time, Pallas kernels for 23%

profile of v2, /device:TPU:0, one launch (start us, length us, event | category | flops | bytes accessed | tf_op | source)
XLA Modules:
  0.0 252.2 jit_solution(1979667778139839533)
XLA Ops:
  0.7 0.9 convert_reduce_fusion
  1.6 0.0 copy-start.2
  1.6 0.5 copy-done.2
  2.1 0.8 select_reduce_fusion
  3.0 0.0 copy-start.4
  3.0 0.0 copy-start.5
  3.0 0.8 copy.30.order_ref
  3.8 0.7 pad_add_fusion.where_ref
  4.5 0.5 multiply_sine_fusion
  5.0 0.8 pad_maximum_fusion
  5.8 16.3 %down_project.1 = (bf16[256,1536]{1,0:T(8,128)(2,1)}, f32[256,512]{1,0:T(8,128)}, f32[256,64]{1,0:T(8,128)}) custom-call(s32[256,1]{1,0:T(8,128)} %copy.30.order_ref, bf16[256,6144]{1,0:T(8,128)(2,1)} %hid_hbm.1, bf16[6144,1536]{1,0:T(8,128)(2,1)} %wdq_ref.1, bf16[576,6144]{1,0:T(8,128)(2,1)} %bitcast.28, bf16[1536]{0:T(1024)(128)(2,1)} %gq_ref.1, ...), custom_call_target="tpu_custom_call" | custom-call | flops 7449083904 | bytes 25952256 | tf_op jit(solution)/shard_map/down_project/pallas_call | solution.py:141
  22.1 0.0 copy-done.4
  22.1 0.0 copy-done.5
  22.1 25.6 %head_queries.1 = (bf16[256,32,512]{2,1,0:T(8,128)(2,1)}, bf16[256,32,64]{2,1,0:T(8,128)(2,1)}) custom-call(bf16[256,1536]{1,0:T(8,128)(2,1)} %get-tuple-element.81.cq_ref, f32[256,64]{1,0:T(8,128)} %get-tuple-element.145.cos_ref, f32[256,64]{1,0:T(8,128)} %get-tuple-element.146.sin_ref, bf16[32,192,1536]{2,1,0:T(8,128)(2,1)} %bitcast.24, ...), custom_call_target="tpu_custom_call" | custom-call | flops 5905580032 | bytes 23068672 | tf_op jit(solution)/shard_map/head_queries/pallas_call | solution.py:83
  47.7 57.9 %attend_chunk_0.1 = (f32[128,16,512]{2,1,0:T(8,128)}, f32[128,16,512]{2,1,0:T(8,128)}, f32[16,128]{1,0:T(8,128)}, f32[16,128]{1,0:T(8,128)}, f32[16,128]{1,0:T(8...) custom-call(s32[256]{0:T(256)} %copy-done.4, s32[256]{0:T(256)} %copy-done.5, ...), custom_call_target="tpu_custom_call" | custom-call | flops 68719476736 | bytes 150994944 | tf_op jit(solution)/shard_map/attend_chunk_0/pallas_call | solution.py:276
  105.6 13.0 %pair_merge_2.1 = (f32[64,16,512]{2,1,0:T(8,128)}, f32[65,16,512]{2,1,0:T(8,128)}, f32[16,128]{1,0:T(8,128)}, f32[16,128]{1,0:T(8,128)}, bf16[16,512,128]{2,1,0:T(8,128)(2,1)}) custom-call(f32[16,128]{1,0:T(8,128)} %get-tuple-element.86.m0_ref, f32[16,128]{1,0:T(8,128)} %get-tuple-element.87.l0_ref, f32[16,128]{1,0:T(8,128)} %get-tuple-element.88.m1_ref, ...), custom_call_target="tpu_custom_call" | custom-call | tf_op jit(solution)/shard_map/pair_merge_2/pallas_call | solution.py:743
  118.7 3.1 %collective-permute-start.6 = (f32[65,16,512]{2,1,0:T(8,128)}, f32[65,16,512]{2,1,0:T(8,128)}, u32[]{:S(2)}, u32[]{:S(2)}) collective-permute-start(f32[65,16,512]{2,1,0:T(8,128)} %get-tuple-element.102), channel_id=1, source_target_pairs={{0,2},{2,0},{1,3},{3,1},{4,6},{6,4},{5,7},{7,5}} | collective-permute-start | bytes 6389768 | tf_op jit(solution)/shard_map/ppermute | solution.py:817
  121.8 0.0 copy-start.6
  121.8 0.0 copy-start.3
  121.8 57.7 %attend_chunk_128.1 = (f32[128,16,512]{2,1,0:T(8,128)}, f32[128,16,512]{2,1,0:T(8,128)}, f32[16,128]{1,0:T(8,128)}, f32[16,128]{1,0:T(8,128)}, f32[16,128]{1,0:T...) custom-call(s32[256]{0:T(256)} %copy-done.4, ...), custom_call_target="tpu_custom_call", output_to_operand_aliasing={{6}: (9, {}), {7}: (10, {})} | custom-call | flops 68719476736 | bytes 150994944 | tf_op jit(solution)/shard_map/attend_chunk_128/pallas_call | solution.py:276
  179.5 0.0 copy-done.6
  179.5 0.5 slice.3
  180.7 0.0 copy-done.3
  180.7 0.6 fusion.7.place_ref
  181.3 0.0 collective-permute-done.6.ux_hbm
  181.3 67.0 %finish_3.1 = bf16[256,6144]{1,0:T(8,128)(2,1)} custom-call(s32[256]{0:T(256)} %fusion.7.place_ref, f32[16,128]{1,0:T(8,128)} %get-tuple-element.92.mk_ref, f32[16,128]{1,0:T(8,128)} %get-tuple-element.93.lk_ref, f32[16,128]{1,0:T(8,128)} %get-tuple-element.106.m0_ref, f32[16,128]{1,0:T(8,128)} %get-tuple-element.107.l0_ref, ...), custom_call_target="tpu_custom_call" | custom-call | tf_op jit(solution)/shard_map/finish_3/pallas_call | solution.py:620
  248.3 3.9 %copy.65 = bf16[256,6144]{1,0:T(8,128)(2,1)} copy(bf16[256,6144]{1,0:T(8,128)(2,1)} %finish_3.1) | data formatting | bytes 6291456
  (3 shorter events, 0.0 us)
Async XLA Ops:
  1.6 0.6 copy-start.2
  3.0 19.1 %copy-start.4 = (s32[256]{0:T(256)}, s32[256]{0:T(256)S(1)}, u32[]{:S(2)}) copy-start(s32[256]{0:T(256)S(1)} %get-tuple-element.118.order_ref) | copy-start | bytes 3076
  3.0 19.1 %copy-start.5 = (s32[256]{0:T(256)}, s32[256]{0:T(256)S(1)}, u32[]{:S(2)}) copy-start(s32[256]{0:T(256)S(1)} %get-tuple-element.117.pos_ref) | copy-start | bytes 3076
  118.7 62.6 %collective-permute-start.6 = (f32[65,16,512]{2,1,0:T(8,128)}, f32[65,16,512]{2,1,0:T(8,128)}, u32[]{:S(2)}, u32[]{:S(2)}) collective-permute-start(f32[65,16,512]{2,1,0:T(8,128)} %get-tuple-element.102), channel_id=1, source_target_pairs={{0,2},{2,0},{1,3},{3,1},{4,6},{6,4},{5,7},{7,5}} | collective-permute-start | bytes 6389768 | tf_op jit(solution)/shard_map/ppermute | solution.py:817
  121.8 57.7 %copy-start.6 = (s32[256]{0:T(256)S(1)}, s32[256]{0:T(256)}, u32[]{:S(2)}) copy-start(s32[256]{0:T(256)} %copy-done.5) | copy-start | bytes 3076
  121.8 58.9 %copy-start.3 = (s32[256]{0:T(256)S(1)}, s32[256]{0:T(256)}, u32[]{:S(2)}) copy-start(s32[256]{0:T(256)} %copy-done.2) | copy-start | bytes 3076

commit v3 on v2

--- a/solution.py
+++ b/solution.py
@@ -15,6 +15,7 @@
 RING = 4
 AHEAD = 2
 VIA_Y = 0
+SHIP = 2
 LANES = 128
 PACK = 16
 VMEM_BYTES = 67043328
@@ -101,7 +102,7 @@
     )(cq, cos2, sin2, w_uq_t, w_uk)
 
 
-def down_kernel(order_ref, hid_ref, wdq_ref, wkv_ref, gq_ref, gkv_ref, cos_ref, sin_ref, cq_ref, latn_ref, ropen_ref, pick, acc_q, acc_kv):
+def down_kernel(rank_ref, hid_ref, wdq_ref, wkv_ref, gq_ref, gkv_ref, cos_ref, sin_ref, cq_ref, latn_ref, ropen_ref, pick, acc_q, acc_kv):
     i = pl.program_id(0)
     rows = hid_ref.shape[0]
     rank = gkv_ref.shape[0]
@@ -109,7 +110,7 @@
 
     @pl.when(i == 0)
     def _():
-        pick[...] = (order_ref[...] == lax.broadcasted_iota(jnp.int32, (rows, rows), 1)).astype(jnp.bfloat16)
+        pick[...] = (rank_ref[...][None, :] == lax.broadcasted_iota(jnp.int32, (rows, rows), 0)).astype(jnp.bfloat16)
         acc_q[...] = jnp.zeros_like(acc_q)
         acc_kv[...] = jnp.zeros_like(acc_kv)
 
@@ -131,7 +132,7 @@
         ropen_ref[...] = (r * cos_ref[...] + turned * sin_ref[...]).astype(jnp.bfloat16).astype(jnp.float32)
 
 
-def down_project(order, hidden, w_dq, w_dkv_t, gain_q, gain_kv, cos2, sin2):
+def down_project(rank_of, hidden, w_dq, w_dkv_t, gain_q, gain_kv, cos2, sin2):
     rows, dmodel = hidden.shape
     qrank = w_dq.shape[1]
     width = w_dkv_t.shape[0]
@@ -142,7 +143,7 @@
         down_kernel,
         grid=(dmodel // block,),
         in_specs=[
-            pl.BlockSpec((rows, 1), fixed),
+            pl.BlockSpec((rows,), lambda i: (0,)),
             pl.BlockSpec((rows, block), lambda i: (0, i)),
             pl.BlockSpec((block, qrank), lambda i: (i, 0)),
             pl.BlockSpec((width, block), lambda i: (0, i)),
@@ -165,7 +166,7 @@
         compiler_params=pltpu.CompilerParams(dimension_semantics=('arbitrary',), vmem_limit_bytes=VMEM_BYTES - 8 * VMEM_STEP),
         cost_estimate=pl.CostEstimate(flops=2 * rows * dmodel * (qrank + width + rows), bytes_accessed=2 * dmodel * (qrank + width), transcendentals=0),
         name='down_project',
-    )(order[:, None], hidden, w_dq, w_dkv_t, gain_q, gain_kv, cos2, sin2)
+    )(rank_of, hidden, w_dq, w_dkv_t, gain_q, gain_kv, cos2, sin2)
 
 
 def attend_kernel(first, steps, scale, order_ref, pos_ref, where_ref, qa_ref, qr_ref, latn_ref, ropen_ref, lat_hbm, rope_hbm, *rest):
@@ -323,8 +324,12 @@
         first = pl.multiple_of((j // half_blocks) * 4 * rows // 2 + ((x * 2 + c) * 2 + t) * r4, r4)
         return full.at[lax.rem(j, half_blocks), pl.ds(first, r4)]
 
-    def send_o():
-        return remote(o2.at[pl.ds(rows, rows)], o_got, o_sem, 0, nbx)
+    pieces = o_sem.shape[-1]
+    share = rows // pieces
+
+    def send_o(k):
+        first = pl.multiple_of(k * share, share)
+        return remote(o2.at[pl.ds(rows + first, share)], o_got.at[pl.ds(first, share)], o_sem, k, nbx)
 
     def copy_c(j):
         return remote(part.at[j, pl.ds(pl.multiple_of((1 - core) * r2, r2), r2)], got_c.at[j], c_sem, j, sib)
@@ -459,9 +464,10 @@
             lax.fori_loop(0, side_b, first_side, 0)
             heads_out(o2, rows)
 
-            @pl.when(xpos == 0)
-            def _():
-                send_o().start()
+        @pl.when(jnp.logical_and(xpos == 0, jnp.logical_and(i >= 1, i <= pieces // SHIP)))
+        def _():
+            for e in range(SHIP):
+                send_o((i - 1) * SHIP + e).start()
 
         @pl.when(jnp.logical_and(i >= 3, i < 5))
         def _():
@@ -483,7 +489,8 @@
         def _():
             @pl.when(jnp.logical_and(j == half_blocks, xpos == 1))
             def _():
-                send_o().wait_recv()
+                for k in range(pieces):
+                    send_o(k).wait_recv()
 
             wcopy(j).wait()
             w = wbuf.at[lax.rem(j, wbuf.shape[0])]
@@ -600,7 +607,8 @@
 
     @pl.when(xpos == 0)
     def _():
-        send_o().wait_send()
+        for k in range(pieces):
+            send_o(k).wait_send()
 
 
 def finish(place, first, second, hidden, wv_heads, w_out, blocks, tag):
@@ -643,7 +651,7 @@
             pltpu.VMEM((batch, dmodel), jnp.bfloat16),
             pltpu.VMEM((batch, dmodel), jnp.bfloat16),
             pltpu.SemaphoreType.DMA((ring,)),
-            pltpu.SemaphoreType.DMA((2, 1, 1)),
+            pltpu.SemaphoreType.DMA((2, 1, 8)),
             *[pltpu.SemaphoreType.DMA((2, 1, blocks))] * 5,
             pltpu.SemaphoreType.DMA((2, 4, blocks)),
             pltpu.SemaphoreType.DMA((2,)),
@@ -659,7 +667,7 @@
     )(place, mk, lk, m0, l0, m1, l1, uk, ux, uo, us, wv_heads, hidden, w_out)
 
 
-def pair_kernel(m0_ref, l0_ref, m1_ref, l1_ref, uo_hbm, us_hbm, wuv_hbm, keep_ref, send_ref, m_ref, l_ref, wvh_ref, got, own, mg, lg, wv, wv_wide, ml_sem, d_sem, o_sem, v_sem):
+def pair_kernel(m0_ref, l0_ref, m1_ref, l1_ref, uo_hbm, us_hbm, wuv_hbm, m_ref, l_ref, keep_hbm, send_hbm, wvh_hbm, got, own, mg, lg, wv, wv_wide, wvh, extra, ml_sem, d_sem, o_sem, v_sem, r_sem, e_sem):
     blocks, rows = own.shape[0], own.shape[1]
     sp = lax.axis_index('sp')
     xpos = sp // 2
@@ -695,7 +703,9 @@
     for p in range(2):
         wv_wide[...] = wv[:, p * quad:(p + 1) * quad, :].astype(jnp.float32)
         for h in range(quad):
-            wvh_ref[p * quad + h] = wv_wide[:, h, :].astype(jnp.bfloat16)
+            wvh[p * quad + h] = wv_wide[:, h, :].astype(jnp.bfloat16)
+    ends = [pltpu.make_async_copy(wvh, wvh_hbm, v_sem), pltpu.make_async_copy(extra, send_hbm.at[blocks * rows // 2], e_sem)]
+    ends[0].start()
     cm.wait()
     cl.wait()
     m0, m1 = m0_ref[...], mg[...]
@@ -705,32 +715,40 @@
     m_ref[...] = m
     l = l0_ref[...] * a0 + lg[...] * a1
     l_ref[...] = l
-    send_ref[blocks * rows // 2] = jnp.concatenate([m, l, m, l], axis=1)
+    extra[...] = jnp.concatenate([m, l, m, l], axis=1)
     lanes = lax.broadcasted_iota(jnp.int32, (1, 128), 1)
 
-    def merge_block(j, out_ref, first):
+    def leave(j, out_hbm, first):
+        return pltpu.make_async_copy(own.at[j], out_hbm.at[pl.ds(first, rows)], r_sem.at[j])
+
+    def merge_block(j, out_hbm, first):
         mine(j).wait()
         theirs(j).wait_recv()
         for r in range(rows):
             hit = lanes == j * rows + r
             c0 = jnp.sum(jnp.where(hit, a0, 0.0), axis=1, keepdims=True)
             c1 = jnp.sum(jnp.where(hit, a1, 0.0), axis=1, keepdims=True)
-            out_ref[first + r] = own[j, r] * c0 + got[j, r] * c1
+            own[j, r] = own[j, r] * c0 + got[j, r] * c1
+        leave(j, out_hbm, first).start()
 
     side = blocks // 2
 
     def body(j, carry):
-        merge_block((1 - xpos) * side + j, send_ref, j * rows)
-        merge_block(xpos * side + j, keep_ref, j * rows)
+        merge_block((1 - xpos) * side + j, send_hbm, j * rows)
+        merge_block(xpos * side + j, keep_hbm, j * rows)
         return carry
 
     lax.fori_loop(0, side, body, 0)
+    ends[1].start()
 
     def drain(j, carry):
         theirs(j).wait_send()
+        leave(j, keep_hbm, 0).wait()
         return carry
 
     lax.fori_loop(0, blocks, drain, 0)
+    for c in ends:
+        c.wait()
 
 
 def pair_merge(mo, lo, ms, ls, uo, us, w_uv, tag):
@@ -743,12 +761,11 @@
     return pl.pallas_call(
         pair_kernel,
         in_specs=[vmem, vmem, vmem, vmem, any_spec, any_spec, any_spec],
-        out_specs=[vmem, vmem, vmem, vmem, vmem],
+        out_specs=[vmem, vmem, any_spec, any_spec, any_spec],
         out_shape=[
+            *[jax.ShapeDtypeStruct((half, LANES), jnp.float32)] * 2,
             jax.ShapeDtypeStruct((count // 2, half, rank), jnp.float32),
             jax.ShapeDtypeStruct((count // 2 + 1, half, rank), jnp.float32),
-            jax.ShapeDtypeStruct((half, LANES), jnp.float32),
-            jax.ShapeDtypeStruct((half, LANES), jnp.float32),
             jax.ShapeDtypeStruct((half, rank, vdim), jnp.bfloat16),
         ],
         scratch_shapes=[
@@ -758,8 +775,12 @@
             pltpu.VMEM((half, LANES), jnp.float32),
             pltpu.VMEM((rank, half, vdim), jnp.bfloat16),
             pltpu.VMEM((rank, half // 2, vdim), jnp.float32),
+            pltpu.VMEM((half, rank, vdim), jnp.bfloat16),
+            pltpu.VMEM((half, rank), jnp.float32),
             pltpu.SemaphoreType.DMA((2, 2)),
             pltpu.SemaphoreType.DMA((2, blocks)),
+            pltpu.SemaphoreType.DMA((blocks,)),
+            pltpu.SemaphoreType.DMA,
             pltpu.SemaphoreType.DMA((blocks,)),
             pltpu.SemaphoreType.DMA,
         ],
@@ -803,7 +824,7 @@
         cos_t, sin_t = rope_tables(pos, rope_cache.shape[2])
         cos2 = jnp.concatenate([cos_t, cos_t], axis=1)
         sin2 = jnp.concatenate([sin_t, sin_t], axis=1)
-        cq, latn, ropen = down_project(order, hidden, w_dq, jnp.transpose(w_dkv), gain_q, gain_kv, cos2, sin2)
+        cq, latn, ropen = down_project(rank_of, hidden, w_dq, jnp.transpose(w_dkv), gain_q, gain_kv, cos2, sin2)
         rope_t = jnp.swapaxes(rope_cache, 1, 2)
         where = jnp.stack([sp * slots, core]).astype(jnp.int32)
         q_abs, q_rope = head_queries(cq, cos2, sin2, jnp.transpose(w_uq, (1, 2, 0)), w_uk)
@@ -812,7 +833,7 @@
         own_rows = rows // 4
         args = (scale, order, pos)
         uo, us, mo, lo, ms, ls, *held = attend_chunk(0, half_rows, *args, where, q_abs, q_rope, latn, ropen, lat_cache, rope_t, [])
-        keep, send, mk, lk, wv_heads = pair_merge(mo, lo, ms, ls, uo, us, w_uv, 2)
+        mk, lk, keep, send, wv_heads = pair_merge(mo, lo, ms, ls, uo, us, w_uv, 2)
         where, send = lax.optimization_barrier((where, send))
         ux = lax.ppermute(send, 'sp', across)
         uo, us, mo, lo, ms, ls, lat_out, rope_n = attend_chunk(half_rows, half_rows, *args, where, q_abs, q_rope, latn, ropen, lat_cache, rope_t, held)

time: 253 us -> 252 us (level)
  no operation moved by 1% of the time
where the time goes in v3:
time: 252 us; the launch traced here: 251 us
  Pallas kernels  237 us (94%)
  other arithmetic  4.98 us (2%)
  local copies, waits for them, and re-layouts  4.41 us (2%)
  starting transfers between devices  3.34 us (1%)
    pallas_call x2, Pallas kernels, attend_chunk(): pl.pallas_call(functools.partial(attend_kernel, first, steps, scale), gri...  116 us
    pallas_call x1, Pallas kernels, finish(): pl.pallas_call(finish_kernel, in_specs=[pl.BlockSpec(memory_space=pltpu.S...  67.2 us
    pallas_call x1, Pallas kernels, head_queries(): pl.pallas_call(heads_kernel, grid=(heads // block,), in_specs=[whole(cq),...  25.5 us
    pallas_call x1, Pallas kernels, down_project(): pl.pallas_call(down_kernel, grid=(dmodel // block,), in_specs=[pl.BlockSp...  16.2 us
    pallas_call x1, Pallas kernels, pair_merge(): pl.pallas_call(pair_kernel, in_specs=[vmem, vmem, vmem, vmem, any_spec, a...  11.9 us
  transfers between devices with their start and end apart: 1, of which 0 were waited for; matrix products, arithmetic and copies ran while one was open for 0% of the time, Pallas kernels for 23%

profile of v3, /device:TPU:0, one launch (start us, length us, event | category | flops | bytes accessed | tf_op | source)
XLA Modules:
  0.0 251.1 jit_solution(14186364206402921755)
XLA Ops:
  0.7 0.9 convert_reduce_fusion.rank_ref
  1.6 0.0 copy-start.2
  1.6 1.4 select_reduce_fusion
  3.0 0.0 copy-start.4
  3.0 0.6 pad_add_fusion.where_ref
  3.7 0.5 multiply_sine_fusion
  4.2 0.8 pad_maximum_fusion
  5.0 0.0 copy-done.2
  5.1 16.2 %down_project.1 = (bf16[256,1536]{1,0:T(8,128)(2,1)}, f32[256,512]{1,0:T(8,128)}, f32[256,64]{1,0:T(8,128)}) custom-call(s32[256]{0:T(256)} %copy-done.2, bf16[256,6144]{1,0:T(8,128)(2,1)} %hid_hbm.1, bf16[6144,1536]{1,0:T(8,128)(2,1)} %wdq_ref.1, bf16[576,6144]{1,0:T(8,128)(2,1)} %bitcast.27, bf16[1536]{0:T(1024)(128)(2,1)} %gq_ref.1, ...), custom_call_target="tpu_custom_call" | custom-call | flops 7449083904 | bytes 25952256 | tf_op jit(solution)/shard_map/down_project/pallas_call | solution.py:142
  21.3 0.0 copy-done.4
  21.3 25.5 %head_queries.1 = (bf16[256,32,512]{2,1,0:T(8,128)(2,1)}, bf16[256,32,64]{2,1,0:T(8,128)(2,1)}) custom-call(bf16[256,1536]{1,0:T(8,128)(2,1)} %get-tuple-element.81.cq_ref, f32[256,64]{1,0:T(8,128)} %get-tuple-element.145.cos_ref, f32[256,64]{1,0:T(8,128)} %get-tuple-element.146.sin_ref, bf16[32,192,1536]{2,1,0:T(8,128)(2,1)} %bitcast.23, ...), custom_call_target="tpu_custom_call" | custom-call | flops 5905580032 | bytes 23068672 | tf_op jit(solution)/shard_map/head_queries/pallas_call | solution.py:84
  46.8 58.2 %attend_chunk_0.1 = (f32[128,16,512]{2,1,0:T(8,128)}, f32[128,16,512]{2,1,0:T(8,128)}, f32[16,128]{1,0:T(8,128)}, f32[16,128]{1,0:T(8,128)}, f32[16,128]{1,0:T(8...) custom-call(s32[256]{0:T(256)} %get-tuple-element.118.order_ref, ...), custom_call_target="tpu_custom_call" | custom-call | flops 68719476736 | bytes 150994944 | tf_op jit(solution)/shard_map/attend_chunk_0/pallas_call | solution.py:277
  105.0 11.9 %pair_merge_2.1 = (f32[16,128]{1,0:T(8,128)}, f32[16,128]{1,0:T(8,128)}, f32[64,16,512]{2,1,0:T(8,128)}, f32[65,16,512]{2,1,0:T(8,128)}, bf16[16,512,128]{2,1,0:T(8,128)(2,1)}) custom-call(f32[16,128]{1,0:T(8,128)} %get-tuple-element.86.m0_ref, f32[16,128]{1,0:T(8,128)} %get-tuple-element.87.l0_ref, f32[16,128]{1,0:T(8,128)} %get-tuple-element.88.m1_ref, ...), custom_call_target="tpu_custom_call" | custom-call | tf_op jit(solution)/shard_map/pair_merge_2/pallas_call | solution.py:761
  116.9 3.3 %collective-permute-start.6 = (f32[65,16,512]{2,1,0:T(8,128)}, f32[65,16,512]{2,1,0:T(8,128)}, u32[]{:S(2)}, u32[]{:S(2)}) collective-permute-start(f32[65,16,512]{2,1,0:T(8,128)} %get-tuple-element.102), channel_id=1, source_target_pairs={{0,2},{2,0},{1,3},{3,1},{4,6},{6,4},{5,7},{7,5}} | collective-permute-start | bytes 6389768 | tf_op jit(solution)/shard_map/ppermute | solution.py:838
  120.2 0.0 copy-start.5
  120.2 0.0 copy-start.3
  120.3 58.0 %attend_chunk_128.1 = (f32[128,16,512]{2,1,0:T(8,128)}, f32[128,16,512]{2,1,0:T(8,128)}, f32[16,128]{1,0:T(8,128)}, f32[16,128]{1,0:T(8,128)}, f32[16,128]{1,0:T...) custom-call(s32[256]{0:T(256)} %get-tuple-element.118.order_ref, ...), custom_call_target="tpu_custom_call", output_to_operand_aliasing={{6}: (9, {}), {7}: (10, {})} | custom-call | flops 68719476736 | bytes 150994944 | tf_op jit(solution)/shard_map/attend_chunk_128/pallas_call | solution.py:277
  178.2 0.0 copy-done.5
  178.2 0.5 slice.3
  179.4 0.0 copy-done.3
  179.4 0.6 fusion.7.place_ref
  180.0 0.0 collective-permute-done.6.ux_hbm
  180.0 67.2 %finish_3.1 = bf16[256,6144]{1,0:T(8,128)(2,1)} custom-call(s32[256]{0:T(256)} %fusion.7.place_ref, f32[16,128]{1,0:T(8,128)} %get-tuple-element.92.mk_ref, f32[16,128]{1,0:T(8,128)} %get-tuple-element.93.lk_ref, f32[16,128]{1,0:T(8,128)} %get-tuple-element.106.m0_ref, f32[16,128]{1,0:T(8,128)} %get-tuple-element.107.l0_ref, ...), custom_call_target="tpu_custom_call" | custom-call | tf_op jit(solution)/shard_map/finish_3/pallas_call | solution.py:628
  247.2 3.9 %copy.59 = bf16[256,6144]{1,0:T(8,128)(2,1)} copy(bf16[256,6144]{1,0:T(8,128)(2,1)} %finish_3.1) | data formatting | bytes 6291456
  (3 shorter events, 0.0 us)
Async XLA Ops:
  1.6 3.5 %copy-start.2 = (s32[256]{0:T(256)}, s32[256]{0:T(256)S(1)}, u32[]{:S(2)}) copy-start(s32[256]{0:T(256)S(1)} %convert_reduce_fusion.rank_ref) | copy-start | bytes 3076
  3.0 18.3 %copy-start.4 = (s32[256]{0:T(256)}, s32[256]{0:T(256)S(1)}, u32[]{:S(2)}) copy-start(s32[256]{0:T(256)S(1)} %get-tuple-element.117.pos_ref) | copy-start | bytes 3076
  116.9 63.1 %collective-permute-start.6 = (f32[65,16,512]{2,1,0:T(8,128)}, f32[65,16,512]{2,1,0:T(8,128)}, u32[]{:S(2)}, u32[]{:S(2)}) collective-permute-start(f32[65,16,512]{2,1,0:T(8,128)} %get-tuple-element.102), channel_id=1, source_target_pairs={{0,2},{2,0},{1,3},{3,1},{4,6},{6,4},{5,7},{7,5}} | collective-permute-start | bytes 6389768 | tf_op jit(solution)/shard_map/ppermute | solution.py:838
  120.2 58.0 %copy-start.5 = (s32[256]{0:T(256)S(1)}, s32[256]{0:T(256)}, u32[]{:S(2)}) copy-start(s32[256]{0:T(256)} %copy-done.4) | copy-start | bytes 3076
  120.2 59.2 %copy-start.3 = (s32[256]{0:T(256)S(1)}, s32[256]{0:T(256)}, u32[]{:S(2)}) copy-start(s32[256]{0:T(256)} %copy-done.2) | copy-start | bytes 3076
